TPU v7x, 32 devices: a whole 2x2x4 slice. The times are simulated.
32 devices in a mesh: groups: 2 (over y), seq: 16 (over z, x, core).
Axes of the slice: x: 2, y: 2, z: 4, core: 2. Of those that a mesh axis runs over, the one named last changes fastest.
Arguments:
- queries: bfloat16 [8192, 2048], P(('groups', 'seq')), parts along dimension 0, may hold values from -20 to 20
- keys: bfloat16 [8192, 2048], P(('groups', 'seq')), parts along dimension 0, may hold values from -20 to 20
- values: bfloat16 [8192, 2048], P(('groups', 'seq')), parts along dimension 0, may hold values from -6 to 6
- block_counts: int32 [16], P('groups'), parts along dimension 0, may hold values from 2 to 6, as said below
- last_tokens: int32 [32], P('groups'), parts along dimension 0, may hold values from 64 to 128
- pack_order: int32 [32], P('groups'), parts along dimension 0, may hold values from 0 to 15, as said below
- decode_slot: int32 [16], P('groups'), parts along dimension 0, may hold values from 0 to 7, each once
Outputs:
- attended: bfloat16 [8192, 2048], P(('groups', 'seq')), parts along dimension 0
- cache_keys: bfloat16 [32, 32, 128, 128], P(('groups', 'seq')), parts along dimension 0
- cache_values: bfloat16 [32, 32, 128, 128], P(('groups', 'seq')), parts along dimension 0
There are 2 independent parts, one for each index of `groups`. A program takes and returns all parts, laid end to end along the dimension named above; each array names one. Nothing has to cross between parts.
Inputs may be any that keep to these rules, and one draw needn't show every extreme that they name: `block_counts`: they sum to 24; the largest equals 6. `pack_order`: each prompt number appears once. The last 1 positions hold null prompts, and the position before them a conditional prompt of 6 blocks. `decode_slot`: each slot appears once.
All inputs are finite; a program needn't handle non-finite values.
Results may differ from a plain program's by a relative error of at most 0.0034.
Values may be sent and summed in bfloat16 or wider, within the bound.
A program may use at most 64 MiB of HBM per device.

v0:
```python
import functools
import math

import jax
import jax.numpy as jnp
from jax import lax
from jax.experimental import pallas as pl
from jax.experimental.pallas import tpu as pltpu
from jax.sharding import PartitionSpec as P

HEADS = 16
HEAD_DIM = 128
BLOCK = 128
MAXB = 6
BACK = MAXB - 1
HIDDEN = -1e30
PLANE = 4
CHUNKS = 4
RELAY = BACK
ROUND = 2


def window_tables(counts_ref, tails_ref, order_ref, first, width):
    pairs = counts_ref.shape[0]
    prompts = order_ref.shape[0]

    def place(i, carry):
        start, docs, valids = carry
        prompt = order_ref[i]
        counted = counts_ref[lax.rem(prompt, pairs)]
        size = jnp.where(prompt < pairs, counted, 1)
        tail = tails_ref[prompt]
        end = start + size
        new_docs, new_valids = [], []
        for w in range(width):
            b = first + w
            inside = (start <= b) & (b < end)
            new_docs.append(jnp.where(inside, i, docs[w]))
            new_valids.append(
                jnp.where(inside, jnp.where(b + 1 == end, tail, BLOCK), valids[w])
            )
        return end, tuple(new_docs), tuple(new_valids)

    none = jnp.int32(-1)
    zero = jnp.int32(0)
    _, docs, valids = lax.fori_loop(
        0, prompts, place, (zero, (none,) * width, (zero,) * width)
    )
    return docs, valids


def exchange(
    n,
    counts_ref,
    tails_ref,
    order_ref,
    q_hbm,
    k_hbm,
    v_hbm,
    out_ref,
    landed_ref,
    q_ref,
    own,
    halo,
    relay,
    bias,
    halo_send,
    halo_recv,
    cache_sem,
    own_sem,
    load_sem,
):
    me = lax.axis_index("seq")
    role = lax.rem(me, PLANE)
    plane = me // PLANE
    planes = n // PLANE
    tokens, features = q_ref.shape
    here = tokens // BLOCK
    splits = n // HEADS
    part = BLOCK // splits
    wide = features // CHUNKS

    loads = [
        pltpu.make_async_copy(src, dst, load_sem.at[i])
        for i, (src, dst) in enumerate(
            ((k_hbm, own.at[0]), (v_hbm, own.at[1]), (q_hbm, q_ref))
        )
    ]
    for copy in loads:
        copy.start()

    barrier = pltpu.get_barrier_semaphore()

    def greet(r, carry):
        pl.semaphore_signal(
            barrier,
            inc=1,
            device_id={"seq": lax.rem(me + r, n)},
            device_id_type=pl.DeviceIdType.MESH,
        )
        return carry

    lax.fori_loop(1, n, greet, 0)
    loads[0].wait()
    loads[1].wait()
    pl.semaphore_wait(barrier, n - 1)

    pending = []

    def spot(block, c):
        return (
            slice(None),
            pl.ds(block * BLOCK, BLOCK),
            pl.ds(c * wide, wide),
        )

    def mine(block):
        return lambda c: own.at[spot(block, c)]

    def held(slot):
        if slot >= RELAY:
            return lambda c: relay.at[spot(slot - RELAY, c)]
        return lambda c: halo.at[spot(slot, c)]

    def start(cond, c, moves):
        copies = []
        for src, target, slot in moves:
            copy = pltpu.make_async_remote_copy(
                src_ref=src(c),
                dst_ref=held(slot)(c),
                send_sem=halo_send.at[len(pending)],
                recv_sem=halo_recv.at[slot, c],
                device_id={"seq": lax.rem(target + n, n)},
                device_id_type=pl.DeviceIdType.MESH,
            )
            pending.append((cond, copy))
            copies.append(copy)

        @pl.when(cond)
        def _():
            for copy in copies:
                copy.start()

    def await_slots(cond, c, slots):
        @pl.when(cond)
        def _():
            for slot in slots:
                ref = held(slot)(c)
                pltpu.make_async_copy(ref, ref, halo_recv.at[slot, c]).wait()

    more = plane < planes - 1
    late = plane > 0
    for c in range(CHUNKS):
        start((role == 3) & more, c, [(mine(0), me + 3, RELAY), (mine(1), me + 3, 0)])
        if c < ROUND:
            moves = [(mine(1), me - 2, RELAY + 1), (mine(0), me - 2, RELAY)]
        else:
            moves = [(mine(1), me + 2, 2), (mine(0), me + 2, 1)]
        start((role == 2) & more, c, moves)
        start((role == 1) & more, c, [(mine(1), me + 3, 0)])
        start(role == 1, c, [(mine(0), me + 1, 3), (mine(1), me + 1, 4)])
        start(role == 0, c, [(mine(1), me + 2, 2), (mine(0), me + 2, 1)])
        start(
            (role == 0) | (role == 2),
            c,
            [(mine(0), me + 1, 3), (mine(1), me + 1, 4)],
        )

    def piece(owner, block):
        head = owner // splits
        cols = pl.ds(pl.multiple_of(head * HEAD_DIM, HEAD_DIM), HEAD_DIM)
        if splits == 1:
            return own.at[:, :, cols]
        offset = pl.multiple_of(block * BLOCK + lax.rem(owner, splits) * part, part)
        return own.at[:, pl.ds(offset, part), cols]

    def place(block):
        if splits == 1:
            return landed_ref.at[:, pl.ds(pl.multiple_of(me * tokens, tokens), tokens)]
        return landed_ref.at[
            :, pl.ds(pl.multiple_of((me * here + block) * part, part), part)
        ]

    pieces = 1 if splits == 1 else here

    def give(s, carry):
        sign = 1 - 2 * lax.rem(s, 2)
        target = lax.rem(me + n // 2 + sign * ((s + 1) // 2), n)
        for block in range(pieces):
            pltpu.make_async_remote_copy(
                src_ref=piece(target, block),
                dst_ref=place(block),
                send_sem=cache_sem.at[0],
                recv_sem=cache_sem.at[1],
                device_id={"seq": target},
                device_id_type=pl.DeviceIdType.MESH,
            ).start()
        return carry

    cuts = [(n - 1) * i // CHUNKS for i in range(CHUNKS + 1)]

    docs, valids = window_tables(
        counts_ref, tails_ref, order_ref, me * here - BACK, BACK + here
    )
    row = lax.broadcasted_iota(jnp.int32, (BLOCK, BLOCK), 0)
    col = lax.broadcasted_iota(jnp.int32, (BLOCK, BLOCK), 1)
    for b in range(here):
        for w in range(BACK + here):
            if w > BACK + b:
                shade = jnp.full((BLOCK, BLOCK), HIDDEN, jnp.float32)
            else:
                limit = jnp.where(docs[w] == docs[BACK + b], valids[w], 0)
                seen = col < limit
                if w == BACK + b:
                    seen = seen & (col <= row)
                shade = jnp.where(seen, 0.0, HIDDEN)
            bias[b * BLOCK : (b + 1) * BLOCK, w * BLOCK : (w + 1) * BLOCK] = shade
    column = lax.broadcasted_iota(jnp.int32, (BLOCK, HEAD_DIM), 0)
    real = jnp.concatenate(
        [column < valids[BACK + b] for b in range(here)], axis=0
    )

    empty = jnp.zeros((BLOCK, features), halo.dtype)
    for slot, reach in ((0, 3), (1, 2), (2, 2), (3, 1), (4, 1)):

        @pl.when(me < reach)
        def _():
            for kv in range(2):
                halo[kv, slot * BLOCK : (slot + 1) * BLOCK, :] = empty

    loads[2].wait()

    factor = HEAD_DIM ** (-0.5) * math.log2(math.e)
    prior = BACK * BLOCK
    nt = (((1,), (1,)), ((), ()))

    def one_head(h, carry):
        cols = pl.ds(pl.multiple_of(h * HEAD_DIM, HEAD_DIM), HEAD_DIM)
        q = q_ref[:, cols]
        s1 = lax.dot_general(q, halo[0, :, cols], nt, preferred_element_type=jnp.float32)
        s2 = lax.dot_general(q, own[0, :, cols], nt, preferred_element_type=jnp.float32)
        s1 = s1 + bias[:, :prior]
        s2 = s2 + bias[:, prior:]
        peak = jnp.maximum(
            jnp.max(s1, axis=1, keepdims=True), jnp.max(s2, axis=1, keepdims=True)
        )
        w1 = jnp.exp2((s1 - peak) * factor)
        w2 = jnp.exp2((s2 - peak) * factor)
        total = jnp.sum(w1, axis=1, keepdims=True) + jnp.sum(w2, axis=1, keepdims=True)
        mixed = jnp.dot(
            w1.astype(jnp.bfloat16), halo[1, :, cols], preferred_element_type=jnp.float32
        ) + jnp.dot(
            w2.astype(jnp.bfloat16), own[1, :, cols], preferred_element_type=jnp.float32
        )
        out_ref[:, cols] = jnp.where(real, mixed / total, 0.0).astype(out_ref.dtype)
        return carry

    for c in range(CHUNKS):
        lax.fori_loop(cuts[c], cuts[c + 1], give, 0)
        if c < ROUND:
            await_slots((role == 0) & more, c, [RELAY, RELAY + 1])
            start(
                (role == 0) & more,
                c,
                [(held(RELAY + 1), me + PLANE, 2), (held(RELAY), me + PLANE, 1)],
            )
        await_slots((role == 2) & late, c, [RELAY, 0])
        start(
            (role == 2) & late, c, [(held(RELAY), me - 2 + n, 3), (held(0), me - 2 + n, 4)]
        )
        await_slots((role == 0) & late, c, [2, 3, 4])
        await_slots(role == 2, c, [2, 3, 4])
        start(
            (role == 2) | ((role == 0) & late),
            c,
            [(held(2), me + 1, 0), (held(3), me + 1, 1), (held(4), me + 1, 2)],
        )
        await_slots((role == 0) & late, c, [0, 1])
        await_slots(role == 1, c, [3, 4])
        await_slots((role == 1) & late, c, [0, 1, 2])
        await_slots(role == 2, c, [1])
        await_slots(role == 3, c, [0, 1, 2, 3, 4])
        each = HEADS // CHUNKS
        lax.fori_loop(c * each, (c + 1) * each, one_head, 0)

    copies = [
        pltpu.make_async_copy(piece(me, block), place(block), own_sem.at[block])
        for block in range(pieces)
    ]
    for copy in copies:
        copy.start()

    for cond, copy in pending:

        @pl.when(cond)
        def _():
            copy.wait_send()

    for copy in copies:
        copy.wait()
    others = landed_ref.shape[1] // n * (n - 1)
    ref = landed_ref.at[:, pl.ds(0, others)]
    pltpu.make_async_copy(ref, ref, cache_sem.at[0]).wait()
    pltpu.make_async_copy(ref, ref, cache_sem.at[1]).wait()


def reorder(
    counts_ref,
    order_ref,
    slot_ref,
    landed_ref,
    mixed_ref,
    attended_ref,
    keys_ref,
    values_ref,
    staged,
    passed,
    who,
    base,
    in_sem,
    out_sem,
):
    enter = pltpu.make_async_copy(mixed_ref, passed, in_sem.at[2])
    enter.start()
    pairs = counts_ref.shape[0]
    prompts = order_ref.shape[0]
    blocks, part = staged.shape[1:3]

    def invert(p, carry):
        who[slot_ref[p]] = p
        return carry

    lax.fori_loop(0, pairs, invert, 0)

    def lay(s, first):
        p = who[s]
        base[p] = first
        return first + counts_ref[p] + 1

    lax.fori_loop(0, pairs, lay, jnp.int32(0))

    def fetch(i, first):
        prompt = order_ref[i]
        pair = lax.rem(prompt, pairs)
        null = prompt >= pairs
        counted = counts_ref[pair]
        size = jnp.where(null, 1, counted)
        target = base[pair] + jnp.where(null, counted, 0)

        def one(w, carry):
            for kv in range(2):
                pltpu.make_async_copy(
                    landed_ref.at[kv, pl.ds((first + w) * part, part)],
                    staged.at[kv, target + w],
                    in_sem.at[kv],
                ).start()
            return carry

        lax.fori_loop(0, size, one, 0)
        return first + size

    lax.fori_loop(0, prompts, fetch, jnp.int32(0))
    enter.wait()
    outs = [pltpu.make_async_copy(passed, attended_ref, out_sem.at[2])]
    outs[0].start()
    for kv, ref in enumerate((keys_ref, values_ref)):
        pltpu.make_async_copy(staged.at[kv], staged.at[kv], in_sem.at[kv]).wait()
        copy = pltpu.make_async_copy(staged.at[kv], ref.at[0], out_sem.at[kv])
        copy.start()
        outs.append(copy)
    for copy in outs:
        copy.wait()


def handoff(
    n,
    counts_ref,
    tails_ref,
    order_ref,
    q_hbm,
    k_hbm,
    v_hbm,
    out_ref,
    landed_ref,
    q_ref,
    own,
    kv,
    qs,
    mixed_ref,
    bias,
    load_sem,
    local_sem,
    kv_send,
    kv_recv,
    q_send,
    q_recv,
    halo_send,
    halo_recv,
    land_send,
    land_recv,
    out_send,
    out_recv,
):
    me = lax.axis_index("seq")
    role = lax.rem(me, PLANE)
    plane = me // PLANE
    planes = n // PLANE
    tokens, features = q_ref.shape
    here = tokens // BLOCK
    width = PLANE * here
    skip = width - BACK
    peers = (role + 1 - 2 * lax.rem(role, 2), lax.rem(role + 2, PLANE), PLANE - 1 - role)
    more = plane < planes - 1
    late = plane > 0

    def rows(first, count):
        return pl.ds(pl.multiple_of(first * BLOCK, BLOCK), count * BLOCK)

    def cols(head):
        return pl.ds(pl.multiple_of(head * HEAD_DIM, HEAD_DIM), HEAD_DIM)

    def remote(src, dst, send, recv, target):
        pltpu.make_async_remote_copy(
            src_ref=src,
            dst_ref=dst,
            send_sem=send,
            recv_sem=recv,
            device_id={"seq": target},
            device_id_type=pl.DeviceIdType.MESH,
        ).start()

    def await_(ref, sem):
        pltpu.make_async_copy(ref, ref, sem).wait()

    mine = rows(BACK + role * here, here)
    place = rows(role * here, here)

    loads = [
        pltpu.make_async_copy(src, dst, load_sem.at[i])
        for i, (src, dst) in enumerate(
            ((k_hbm, own.at[0]), (v_hbm, own.at[1]), (q_hbm, q_ref))
        )
    ]
    loads[0].start()
    loads[1].start()
    for j in range(planes):
        here_cols = cols(j * PLANE + role)
        for i, src in enumerate((k_hbm, v_hbm)):
            pltpu.make_async_copy(
                src.at[:, here_cols], kv.at[j, i, mine], local_sem.at[0]
            ).start()
    loads[2].start()
    for j in range(planes):
        here_cols = cols(j * PLANE + role)
        pltpu.make_async_copy(
            q_hbm.at[:, here_cols], qs.at[j, place], local_sem.at[1]
        ).start()

    barrier = pltpu.get_barrier_semaphore()
    base = plane * PLANE
    for peer in peers:
        pl.semaphore_signal(
            barrier,
            inc=1,
            device_id={"seq": base + peer},
            device_id_type=pl.DeviceIdType.MESH,
        )
    for step in range(1, planes):
        pl.semaphore_signal(
            barrier,
            inc=1,
            device_id={"seq": lax.rem(me + step * PLANE, n)},
            device_id_type=pl.DeviceIdType.MESH,
        )

    loads[0].wait()
    loads[1].wait()
    pl.semaphore_wait(barrier, PLANE - 1 + planes - 1)

    def share(t, carry):
        j = planes - 1 - t
        for k in (1, 2, 0):
            head = j * PLANE + peers[k]
            remote(
                own.at[:, :, cols(head)],
                kv.at[j, :, mine],
                kv_send.at[0],
                kv_recv.at[k, j],
                base + peers[k],
            )
        return carry

    lax.fori_loop(0, planes, share, 0)
    loads[2].wait()

    def share_q(t, carry):
        j = planes - 1 - t
        for k in (1, 2, 0):
            head = j * PLANE + peers[k]
            remote(
                q_ref.at[:, cols(head)],
                qs.at[j, place],
                q_send.at[0],
                q_recv.at[k, j],
                base + peers[k],
            )
        return carry

    lax.fori_loop(0, planes, share_q, 0)

    def forward(j, rho):
        first = BACK + rho * here

        @pl.when(more & (rho * here >= skip))
        def _():
            remote(
                kv.at[j, :, rows(first, here)],
                kv.at[j, :, rows(jnp.maximum(rho * here - skip, 0), here)],
                halo_send.at[0],
                halo_recv.at[j, rho],
                me + PLANE,
            )

        @pl.when(more & (rho * here < skip) & (rho * here + here > skip))
        def _():
            remote(
                kv.at[j, :, rows(BACK + skip, BACK % here)],
                kv.at[j, :, rows(0, BACK % here)],
                halo_send.at[0],
                halo_recv.at[j, rho],
                me + PLANE,
            )

        @pl.when(j < plane)
        def _():
            remote(
                kv.at[j, :, rows(first, here)],
                landed_ref.at[:, rows(plane * width + rho * here, here)],
                land_send.at[0, j],
                land_recv.at[0],
                j * PLANE + role,
            )

    await_(kv.at[:, :, mine], local_sem.at[0])

    def forward_mine(t, carry):
        forward(planes - 1 - t, role)
        return carry

    lax.fori_loop(0, planes, forward_mine, 0)

    def take(k):
        def body(t, carry):
            j = planes - 1 - t
            await_(kv.at[j, :, rows(BACK + peers[k] * here, here)], kv_recv.at[k, j])
            forward(j, peers[k])
            return carry

        return body

    lax.fori_loop(0, planes, take(0), 0)

    docs, valids = window_tables(
        counts_ref, tails_ref, order_ref, plane * width - BACK, BACK + width
    )
    row = lax.broadcasted_iota(jnp.int32, (BLOCK, BLOCK), 0)
    col = lax.broadcasted_iota(jnp.int32, (BLOCK, BLOCK), 1)
    for i in range(PLANE):
        for b in range(here):
            target = BACK + i * here + b
            for w in range(BACK + here):
                if w > BACK + b:
                    shade = jnp.full((BLOCK, BLOCK), HIDDEN, jnp.float32)
                else:
                    source = i * here + w
                    limit = jnp.where(docs[source] == docs[target], valids[source], 0)
                    seen = col < limit
                    if w == BACK + b:
                        seen = seen & (col <= row)
                    shade = jnp.where(seen, 0.0, HIDDEN)
                bias[i, b * BLOCK : (b + 1) * BLOCK, w * BLOCK : (w + 1) * BLOCK] = shade
    column = lax.broadcasted_iota(jnp.int32, (BLOCK, HEAD_DIM), 0)

    @pl.when(plane == 0)
    def _():
        empty = jnp.zeros((planes, 2, BACK * BLOCK, HEAD_DIM), kv.dtype)
        kv[:, :, : BACK * BLOCK, :] = empty

    def take_both(t, carry):
        take(1)(t, carry)
        take(2)(t, carry)
        return carry

    lax.fori_loop(0, planes, take_both, 0)

    def climb(t, carry):
        j = planes - 1 - t

        @pl.when(j > plane)
        def _():
            remote(
                kv.at[j, :, rows(BACK, skip)],
                landed_ref.at[:, rows(plane * width, skip)],
                land_send.at[1, j],
                land_recv.at[0],
                j * PLANE + role,
            )

        return carry

    lax.fori_loop(0, planes, climb, 0)
    settle = pltpu.make_async_copy(
        kv.at[plane, :, rows(BACK, width)],
        landed_ref.at[:, rows(plane * width, width)],
        load_sem.at[0],
    )
    settle.start()
    await_(qs.at[:, place], local_sem.at[1])

    factor = HEAD_DIM ** (-0.5) * math.log2(math.e)
    nt = (((1,), (1,)), ((), ()))
    span = (BACK + here) * BLOCK

    def attend(j, i):
        window = pl.ds(i * tokens, span)
        q = qs[j, pl.ds(i * tokens, tokens), :]
        s = lax.dot_general(q, kv[j, 0, window, :], nt, preferred_element_type=jnp.float32)
        s = s + bias[i]
        peak = jnp.max(s, axis=1, keepdims=True)
        w = jnp.exp2((s - peak) * factor)
        total = jnp.sum(w, axis=1, keepdims=True)
        mixed = jnp.dot(
            w.astype(jnp.bfloat16), kv[j, 1, window, :], preferred_element_type=jnp.float32
        )
        real = jnp.concatenate(
            [column < valids[BACK + i * here + b] for b in range(here)], axis=0
        )
        mixed_ref[j, i] = jnp.where(real, mixed / total, 0.0).astype(mixed_ref.dtype)

    def give(j, i):
        target = out_ref.at[:, cols(j * PLANE + role)]

        @pl.when(role == i)
        def _():
            pltpu.make_async_copy(mixed_ref.at[j, i], target, local_sem.at[2]).start()

        @pl.when(role != i)
        def _():
            remote(mixed_ref.at[j, i], target, out_send.at[0], out_recv.at[0], base + i)

    def one_head(t, carry):
        j = planes - 1 - t
        for k in range(PLANE - 1):
            await_(qs.at[j, rows(peers[k] * here, here)], q_recv.at[k, j])
        attend(j, PLANE - 1)

        @pl.when(t > 0)
        def _():
            give(jnp.minimum(j + 1, planes - 1), 0)

        @pl.when(late)
        def _():
            for rho in range(PLANE):
                count = min(here, (rho + 1) * here - skip)
                if count > 0:
                    await_(
                        kv.at[j, :, rows(max(rho * here - skip, 0), count)],
                        halo_recv.at[j, rho],
                    )

        @pl.when(late & (j > plane))
        def _():
            remote(
                kv.at[j, :, rows(0, BACK)],
                landed_ref.at[:, rows(jnp.maximum(plane * width - BACK, 0), BACK)],
                land_send.at[2, j],
                land_recv.at[0],
                j * PLANE + role,
            )

        for i in range(PLANE - 2, -1, -1):
            attend(j, i)
            give(j, i + 1)
        return carry

    lax.fori_loop(0, planes, one_head, 0)

    settled = pltpu.make_async_copy(
        kv.at[plane, :, rows(0, BACK)],
        landed_ref.at[:, rows(jnp.maximum(plane * width - BACK, 0), BACK)],
        load_sem.at[1],
    )

    @pl.when(late)
    def _():
        settled.start()

    give(0, 0)

    others = features // PLANE * (PLANE - 1)
    await_(own.at[:, :, pl.ds(0, others)], kv_send.at[0])
    await_(q_ref.at[:, pl.ds(0, others)], q_send.at[0])
    await_(q_ref.at[:, pl.ds(0, features // PLANE)], local_sem.at[2])

    @pl.when(more)
    def _():
        await_(kv.at[:, :, rows(0, BACK)], halo_send.at[0])

    def drain(j, carry):
        @pl.when(j < plane)
        def _():
            await_(kv.at[j, :, rows(BACK, width)], land_send.at[0, j])

        @pl.when(j > plane)
        def _():
            await_(kv.at[j, :, rows(BACK, skip)], land_send.at[1, j])

        @pl.when(late & (j > plane))
        def _():
            await_(kv.at[j, :, rows(0, BACK)], land_send.at[2, j])

        return carry

    lax.fori_loop(0, planes, drain, 0)
    settle.wait()

    @pl.when(late)
    def _():
        settled.wait()
        await_(landed_ref.at[:, rows(0, (planes - 1) * width - BACK)], land_recv.at[0])

    @pl.when(plane == 0)
    def _():
        await_(landed_ref.at[:, rows(0, (planes - 1) * width)], land_recv.at[0])

    await_(q_ref.at[:, pl.ds(0, others)], out_send.at[0])
    await_(q_ref.at[:, pl.ds(0, others)], out_recv.at[0])


def wide_exchange(n, queries, keys, values, block_counts, last_tokens, pack_order):
    tokens, features = queries.shape
    here = tokens // BLOCK
    part = BLOCK // (n // HEADS)
    blocks = here * n
    kind = queries.dtype
    smem = pl.BlockSpec(memory_space=pltpu.SMEM)
    vmem = pl.BlockSpec(memory_space=pltpu.VMEM)
    anywhere = pl.BlockSpec(memory_space=pl.ANY)
    dma = pltpu.SemaphoreType.DMA
    return pl.pallas_call(
        functools.partial(exchange, n),
        out_shape=(
            jax.ShapeDtypeStruct((tokens, features), kind),
            jax.ShapeDtypeStruct((2, blocks * part, HEAD_DIM), kind),
        ),
        in_specs=[smem] * 3 + [anywhere] * 3,
        out_specs=(vmem, anywhere),
        scratch_shapes=[
            pltpu.VMEM((tokens, features), kind),
            pltpu.VMEM((2, tokens, features), kind),
            pltpu.VMEM((2, BACK * BLOCK, features), kind),
            pltpu.VMEM((2, 2 * BLOCK, features), kind),
            pltpu.VMEM((tokens, (BACK + here) * BLOCK), jnp.float32),
            dma((CHUNKS * 18,)),
            dma((BACK + 2, CHUNKS)),
            dma((2,)),
            dma((here,)),
            dma((3,)),
        ],
        compiler_params=pltpu.CompilerParams(
            collective_id=0, has_side_effects=True, vmem_limit_bytes=60 * 1024 * 1024
        ),
    )(block_counts, last_tokens, pack_order, queries, keys, values)


def local(n, queries, keys, values, block_counts, last_tokens, pack_order, decode_slot):
    tokens, features = queries.shape
    here = tokens // BLOCK
    splits = n // HEADS
    part = BLOCK // splits
    blocks = here * n
    kind = queries.dtype
    smem = pl.BlockSpec(memory_space=pltpu.SMEM)
    anywhere = pl.BlockSpec(memory_space=pl.ANY)
    dma = pltpu.SemaphoreType.DMA
    planes = n // PLANE
    if splits == 1 and here == 2 and planes > 1:
        attended, landed = pl.pallas_call(
            functools.partial(handoff, n),
            out_shape=(
                jax.ShapeDtypeStruct((tokens, features), kind),
                jax.ShapeDtypeStruct((2, blocks * part, HEAD_DIM), kind),
            ),
            in_specs=[smem] * 3 + [anywhere] * 3,
            out_specs=(anywhere, anywhere),
            scratch_shapes=[
                pltpu.VMEM((tokens, features), kind),
                pltpu.VMEM((2, tokens, features), kind),
                pltpu.VMEM((planes, 2, (BACK + PLANE * here) * BLOCK, HEAD_DIM), kind),
                pltpu.VMEM((planes, PLANE * tokens, HEAD_DIM), kind),
                pltpu.VMEM((planes, PLANE, tokens, HEAD_DIM), kind),
                pltpu.VMEM((PLANE, tokens, (BACK + here) * BLOCK), jnp.float32),
                dma((3,)),
                dma((3,)),
                dma((1,)),
                dma((PLANE - 1, planes)),
                dma((1,)),
                dma((PLANE - 1, planes)),
                dma((1,)),
                dma((planes, PLANE)),
                dma((3, planes)),
                dma((1,)),
                dma((1,)),
                dma((1,)),
            ],
            compiler_params=pltpu.CompilerParams(
                collective_id=0, has_side_effects=True, vmem_limit_bytes=60 * 1024 * 1024
            ),
        )(block_counts, last_tokens, pack_order, queries, keys, values)
    else:
        attended, landed = wide_exchange(
            n, queries, keys, values, block_counts, last_tokens, pack_order
        )
    cache = jax.ShapeDtypeStruct((1, blocks, part, HEAD_DIM), kind)
    attended, cache_keys, cache_values = pl.pallas_call(
        reorder,
        out_shape=(jax.ShapeDtypeStruct((tokens, features), kind), cache, cache),
        in_specs=[smem] * 3 + [anywhere] * 2,
        out_specs=(anywhere,) * 3,
        scratch_shapes=[
            pltpu.VMEM((2, blocks, part, HEAD_DIM), kind),
            pltpu.VMEM((tokens, features), kind),
            pltpu.SMEM(block_counts.shape, jnp.int32),
            pltpu.SMEM(block_counts.shape, jnp.int32),
            dma((3,)),
            dma((3,)),
        ],
    )(block_counts, pack_order, decode_slot, landed, attended)
    return attended, cache_keys, cache_values


def solution(mesh):
    rows = P(("groups", "seq"), None)
    small = P("groups")
    cache = P(("groups", "seq"), None, None, None)
    return jax.shard_map(
        functools.partial(local, mesh.shape["seq"]),
        mesh=mesh,
        in_specs=(rows, rows, rows, small, small, small, small),
        out_specs=(rows, cache, cache),
        check_vma=False,
    )
```

profile of v0, /device:TPU:18, one launch (start us, length us, event | category | flops | bytes accessed | tf_op | source)
XLA Modules:
  0.0 68.6 jit_solution(13685248049631559208)
XLA Ops:
  0.6 64.1 %shard_map.94 = (bf16[256,2048]{1,0:T(8,128)(2,1)}, bf16[2,4096,128]{2,1,0:T(8,128)(2,1)}) custom-call(s32[8]{0:T(128)} %counts_ref.3, s32[16]{0:T(128)} %tails_ref.1, s32[16]{0:T(128)} %order_ref.3, bf16[256,2048]{1,0:T(8,128)(2,1)} %q_hbm.1, bf16[256,2048]{1,0:T(8,128)(2,1)} %k_hbm.1, bf16[256,2048]{1,0:T(8,128)(2,1)} %v_hbm.1), custom_call_target="tpu_custom_call" | custom-call | tf_op jit(solution)/shard_map/pallas_call | solution.py:788
  64.7 3.9 %shard_map.95 = (bf16[256,2048]{1,0:T(8,128)(2,1)}, bf16[1,32,128,128]{3,2,1,0:T(8,128)(2,1)}, bf16[1,32,128,128]{3,2,1,0:T(8,128)(2,1)}) custom-call(s32[8]{0:T(128)} %counts_ref.3, s32[16]{0:T(128)} %order_ref.3, s32[8]{0:T(128)} %slot_ref.1, bf16[2,4096,128]{2,1,0:T(8,128)(2,1)} %get-tuple-element.5.landed_ref, bf16[256,2048]{1,0:T(8,128)(2,1)} %get-tuple-element.6.mixed_ref), custom_call_target="tpu_custom_call" | custom-call | tf_op jit(solution)/shard_map/pallas_call | solution.py:825
where the time goes:
time: 68.8 us; the launch traced here: 68.6 us
  Pallas kernels  68 us (99%)
    pallas_call x1, Pallas kernels, local(): pl.pallas_call(functools.partial(handoff, n), out_shape=(jax.ShapeDtypeSt...  64.1 us
    pallas_call x1, Pallas kernels, local(): pl.pallas_call(reorder, out_shape=(jax.ShapeDtypeStruct((tokens, features...  3.9 us

commit v1 on v0

--- a/solution.py
+++ b/solution.py
@@ -388,6 +388,12 @@
     qs,
     mixed_ref,
     bias,
+    lower_q,
+    lower_bias,
+    part_out,
+    part_in,
+    size_out,
+    size_in,
     load_sem,
     local_sem,
     kv_send,
@@ -400,6 +406,10 @@
     land_recv,
     out_send,
     out_recv,
+    down_send,
+    down_recv,
+    up_send,
+    up_recv,
 ):
     me = lax.axis_index("seq")
     role = lax.rem(me, PLANE)
@@ -409,9 +419,50 @@
     here = tokens // BLOCK
     width = PLANE * here
     skip = width - BACK
+    reach = BACK * BLOCK
     peers = (role + 1 - 2 * lax.rem(role, 2), lax.rem(role + 2, PLANE), PLANE - 1 - role)
     more = plane < planes - 1
     late = plane > 0
+    base = plane * PLANE
+    last = planes - 1
+    orders = []
+    for p in range(planes):
+        above = list(range(last, p, -1))
+        helping = [j for j in range(p + 1) if j + p < last and 2 * p >= planes - 2]
+        rest = [j for j in range(p, -1, -1) if j not in helping]
+        if p == last:
+            above, helping, rest = [last - 1], list(range(last - 1)), [last]
+        orders.append(above + helping + rest)
+    def one_if(i, value):
+        return (i + planes - value) // planes - (i + planes - value - 1) // planes
+
+    picks = [
+        sum(orders[p][t] * one_if(plane, p) for p in range(planes)) for t in range(planes)
+    ]
+
+    def turn(t):
+        return sum(picks[other] * one_if(t, other) for other in range(planes))
+
+    def hold(j):
+        return ((plane == last) & (j < plane - 1)) | ((plane == 0) & (j < planes // 2))
+
+    def back(j, p):
+        return (j <= p) & (j + p < planes - 1) & (2 * p >= planes - 2)
+
+    helpable = sorted({j for p in range(last) for j in range(p + 1) if j + p < last and 2 * p >= planes - 2})
+
+    def helps(j):
+        return more & back(j, plane)
+
+    def helped(j):
+        return late & back(j, plane - 1)
+
+    def each(body):
+        def step(t, carry):
+            body(turn(t))
+            return carry
+
+        lax.fori_loop(0, planes, step, 0)
 
     def rows(first, count):
         return pl.ds(pl.multiple_of(first * BLOCK, BLOCK), count * BLOCK)
@@ -441,15 +492,14 @@
             ((k_hbm, own.at[0]), (v_hbm, own.at[1]), (q_hbm, q_ref))
         )
     ]
-    loads[0].start()
-    loads[1].start()
+    for load in loads:
+        load.start()
     for j in range(planes):
         here_cols = cols(j * PLANE + role)
         for i, src in enumerate((k_hbm, v_hbm)):
             pltpu.make_async_copy(
                 src.at[:, here_cols], kv.at[j, i, mine], local_sem.at[0]
             ).start()
-    loads[2].start()
     for j in range(planes):
         here_cols = cols(j * PLANE + role)
         pltpu.make_async_copy(
@@ -457,7 +507,6 @@
         ).start()
 
     barrier = pltpu.get_barrier_semaphore()
-    base = plane * PLANE
     for peer in peers:
         pl.semaphore_signal(
             barrier,
@@ -473,62 +522,101 @@
             device_id_type=pl.DeviceIdType.MESH,
         )
 
-    loads[0].wait()
-    loads[1].wait()
-    pl.semaphore_wait(barrier, PLANE - 1 + planes - 1)
-
-    def share(t, carry):
-        j = planes - 1 - t
+    for j in range(planes):
+
+        @pl.when((plane == 0) | helped(j))
+        def _():
+            for i in range(2):
+                kv[j, i, :reach, :] = jnp.zeros((reach, HEAD_DIM), kv.dtype)
+
+    with jax.named_scope("enter"):
+        for load in loads:
+            load.wait()
+        pl.semaphore_wait(barrier, PLANE - 1 + planes - 1)
+
+    def share(j):
         for k in (1, 2, 0):
-            head = j * PLANE + peers[k]
             remote(
-                own.at[:, :, cols(head)],
+                own.at[:, :, cols(j * PLANE + peers[k])],
                 kv.at[j, :, mine],
                 kv_send.at[0],
                 kv_recv.at[k, j],
                 base + peers[k],
             )
-        return carry
-
-    lax.fori_loop(0, planes, share, 0)
-    loads[2].wait()
-
-    def share_q(t, carry):
-        j = planes - 1 - t
+
+    def share_q(j):
         for k in (1, 2, 0):
-            head = j * PLANE + peers[k]
             remote(
-                q_ref.at[:, cols(head)],
+                q_ref.at[:, cols(j * PLANE + peers[k])],
                 qs.at[j, place],
                 q_send.at[0],
                 q_recv.at[k, j],
                 base + peers[k],
             )
-        return carry
-
-    lax.fori_loop(0, planes, share_q, 0)
+
+    def when_helped(body, truth):
+        def step(j):
+            @pl.when(helped(j) if truth else jnp.logical_not(helped(j)))
+            def _():
+                body(j)
+
+        return step
+
+    def descend(body):
+        def step(t, carry):
+            body(last - t)
+            return carry
+
+        lax.fori_loop(0, planes, step, 0)
+
+    each(when_helped(share_q, True))
+    each(share)
+    descend(when_helped(share_q, False))
 
     def forward(j, rho):
         first = BACK + rho * here
-
-        @pl.when(more & (rho * here >= skip))
+        low = rho * here < skip
+        high = rho * here + here > skip
+        up = more & jnp.logical_not(helps(j))
+
+        @pl.when(up & jnp.logical_not(low))
         def _():
             remote(
                 kv.at[j, :, rows(first, here)],
                 kv.at[j, :, rows(jnp.maximum(rho * here - skip, 0), here)],
-                halo_send.at[0],
+                halo_send.at[j],
                 halo_recv.at[j, rho],
                 me + PLANE,
             )
 
-        @pl.when(more & (rho * here < skip) & (rho * here + here > skip))
+        @pl.when(up & low & high)
         def _():
             remote(
                 kv.at[j, :, rows(BACK + skip, BACK % here)],
                 kv.at[j, :, rows(0, BACK % here)],
-                halo_send.at[0],
+                halo_send.at[j],
                 halo_recv.at[j, rho],
                 me + PLANE,
+            )
+
+        @pl.when(late & (j > plane) & low & high)
+        def _():
+            remote(
+                kv.at[j, :, rows(first, skip % here)],
+                landed_ref.at[:, rows(plane * width + rho * here, skip % here)],
+                land_send.at[1, j],
+                land_recv.at[0],
+                j * PLANE + role,
+            )
+
+        @pl.when(late & (j > plane) & jnp.logical_not(high))
+        def _():
+            remote(
+                kv.at[j, :, rows(first, here)],
+                landed_ref.at[:, rows(plane * width + rho * here, here)],
+                land_send.at[1, j],
+                land_recv.at[0],
+                j * PLANE + role,
             )
 
         @pl.when(j < plane)
@@ -541,66 +629,185 @@
                 j * PLANE + role,
             )
 
+    def start_mine(j):
+        @pl.when(jnp.logical_not(hold(j)))
+        def _():
+            forward(j, role)
+
+    def take(k, j):
+        await_(kv.at[j, :, rows(BACK + peers[k] * here, here)], kv_recv.at[k, j])
+
+    def start_core(truth):
+        def body(j):
+            @pl.when(helped(j) if truth else jnp.logical_not(helped(j)))
+            def _():
+                take(0, j)
+
+                @pl.when(jnp.logical_not(hold(j)))
+                def _():
+                    forward(j, peers[0])
+
+        return body
+
     await_(kv.at[:, :, mine], local_sem.at[0])
-
-    def forward_mine(t, carry):
-        forward(planes - 1 - t, role)
+    each(start_mine)
+
+    with jax.named_scope("take_core"):
+        each(start_core(False))
+
+    with jax.named_scope("tables"):
+        docs, valids = window_tables(
+            counts_ref, tails_ref, order_ref, plane * width - BACK, BACK + width + BACK
+        )
+        row = lax.broadcasted_iota(jnp.int32, (BLOCK, BLOCK), 0)
+        col = lax.broadcasted_iota(jnp.int32, (BLOCK, BLOCK), 1)
+        hidden = jnp.full((BLOCK, BLOCK), HIDDEN, jnp.float32)
+
+        def shade(source, target):
+            limit = jnp.where(docs[source] == docs[target], valids[source], 0)
+            seen = col < limit
+            if source == target:
+                seen = seen & (col <= row)
+            return jnp.where(seen, 0.0, HIDDEN)
+
+        for i in range(PLANE):
+            for b in range(here):
+                target = BACK + i * here + b
+                for w in range(BACK + here):
+                    source = i * here + w
+                    spot = (slice(b * BLOCK, (b + 1) * BLOCK), slice(w * BLOCK, (w + 1) * BLOCK))
+                    full = hidden if source > target else shade(source, target)
+                    bias[(0, i) + spot] = full
+                    bias[(1, i) + spot] = hidden if source < BACK else full
+        for g in range(BACK):
+            for c in range(BACK):
+                lower_bias[g * BLOCK : (g + 1) * BLOCK, c * BLOCK : (c + 1) * BLOCK] = shade(
+                    BACK + skip + c, BACK + width + g
+                )
+        column = lax.broadcasted_iota(jnp.int32, (BLOCK, HEAD_DIM), 0)
+
+    def await_q(j):
+        for k in range(PLANE - 1):
+            await_(qs.at[j, rows(peers[k] * here, here)], q_recv.at[k, j])
+
+    await_(qs.at[:, place], local_sem.at[1])
+
+    def lower(j):
+        await_q(j)
+        remote(
+            qs.at[j, pl.ds(0, reach)],
+            lower_q.at[j],
+            down_send.at[j],
+            down_recv.at[j],
+            me - PLANE,
+        )
+
+    with jax.named_scope("lower_q"):
+        for h in helpable:
+
+            @pl.when(helped(h))
+            def _():
+                lower(h)
+
+    each(start_core(True))
+
+    def await_halo(j):
+        for rho in range(PLANE):
+            count = min(here, (rho + 1) * here - skip)
+            if count > 0:
+                await_(
+                    kv.at[j, :, rows(max(rho * here - skip, 0), count)],
+                    halo_recv.at[j, rho],
+                )
+
+    below = rows(jnp.maximum(plane * width - BACK, 0), BACK)
+
+    def relay(j):
+        @pl.when(late & (j > plane))
+        def _():
+            await_halo(j)
+            remote(
+                kv.at[j, :, rows(0, BACK)],
+                landed_ref.at[:, below],
+                land_send.at[2, j],
+                land_recv.at[0],
+                j * PLANE + role,
+            )
+
+    factor = HEAD_DIM ** (-0.5) * math.log2(math.e)
+    nt = (((1,), (1,)), ((), ()))
+    span = (BACK + here) * BLOCK
+
+    def soften(q, k, v, mask):
+        s = lax.dot_general(q, k, nt, preferred_element_type=jnp.float32) + mask
+        peak = jnp.max(s, axis=1, keepdims=True)
+        w = jnp.exp2((s - peak) * factor)
+        total = jnp.sum(w, axis=1, keepdims=True)
+        mixed = jnp.dot(w.astype(jnp.bfloat16), v, preferred_element_type=jnp.float32)
+        return mixed, peak * factor, total
+
+    def help_out(j):
+        await_(lower_q.at[j], down_recv.at[j])
+        for first in range(0, BACK, here):
+            count = min(here, BACK - first)
+            lines = slice(first * BLOCK, (first + count) * BLOCK)
+            window = pl.ds((BACK + skip + first) * BLOCK, (BACK - first) * BLOCK)
+            mixed, peak, total = soften(
+                lower_q[j, lines, :],
+                kv[j, 0, window, :],
+                kv[j, 1, window, :],
+                lower_bias[lines, first * BLOCK :],
+            )
+            part_out[j, lines, :] = (mixed / total).astype(part_out.dtype)
+            size = jnp.broadcast_to(peak + jnp.log2(total), (count * BLOCK, BLOCK))
+            for b in range(count):
+                turned = size[b * BLOCK : (b + 1) * BLOCK].T
+                size_out[j, first + b] = turned[:8]
+
+    def send_up(j):
+        remote(part_out.at[j], part_in.at[j], up_send.at[0, j], up_recv.at[0, j], me + PLANE)
+        remote(size_out.at[j], size_in.at[j], up_send.at[1, j], up_recv.at[1, j], me + PLANE)
+
+    def release(j):
+        @pl.when(hold(j))
+        def _():
+            forward(j, role)
+            forward(j, peers[0])
+
+    def far(t, carry):
+        j = turn(t)
+        with jax.named_scope("take_far"):
+            for k in (1, 2):
+                take(k, j)
+                forward(j, peers[k])
+
+        @pl.when(t == min(1, last))
+        def _():
+            each(release)
+
+        for h in helpable:
+
+            @pl.when(helps(h) & (j == h))
+            def _():
+                with jax.named_scope("help_out"):
+                    help_out(h)
+
+        for h in helpable:
+
+            @pl.when(helps(h) & (j == h))
+            def _():
+                send_up(h)
+
         return carry
 
-    lax.fori_loop(0, planes, forward_mine, 0)
-
-    def take(k):
-        def body(t, carry):
-            j = planes - 1 - t
-            await_(kv.at[j, :, rows(BACK + peers[k] * here, here)], kv_recv.at[k, j])
-            forward(j, peers[k])
-            return carry
-
-        return body
-
-    lax.fori_loop(0, planes, take(0), 0)
-
-    docs, valids = window_tables(
-        counts_ref, tails_ref, order_ref, plane * width - BACK, BACK + width
-    )
-    row = lax.broadcasted_iota(jnp.int32, (BLOCK, BLOCK), 0)
-    col = lax.broadcasted_iota(jnp.int32, (BLOCK, BLOCK), 1)
-    for i in range(PLANE):
-        for b in range(here):
-            target = BACK + i * here + b
-            for w in range(BACK + here):
-                if w > BACK + b:
-                    shade = jnp.full((BLOCK, BLOCK), HIDDEN, jnp.float32)
-                else:
-                    source = i * here + w
-                    limit = jnp.where(docs[source] == docs[target], valids[source], 0)
-                    seen = col < limit
-                    if w == BACK + b:
-                        seen = seen & (col <= row)
-                    shade = jnp.where(seen, 0.0, HIDDEN)
-                bias[i, b * BLOCK : (b + 1) * BLOCK, w * BLOCK : (w + 1) * BLOCK] = shade
-    column = lax.broadcasted_iota(jnp.int32, (BLOCK, HEAD_DIM), 0)
-
-    @pl.when(plane == 0)
-    def _():
-        empty = jnp.zeros((planes, 2, BACK * BLOCK, HEAD_DIM), kv.dtype)
-        kv[:, :, : BACK * BLOCK, :] = empty
-
-    def take_both(t, carry):
-        take(1)(t, carry)
-        take(2)(t, carry)
-        return carry
-
-    lax.fori_loop(0, planes, take_both, 0)
-
-    def climb(t, carry):
-        j = planes - 1 - t
-
-        @pl.when(j > plane)
+    lax.fori_loop(0, planes, far, 0)
+
+    def climb(j, carry):
+        @pl.when((plane == 0) & (j > 0))
         def _():
             remote(
                 kv.at[j, :, rows(BACK, skip)],
-                landed_ref.at[:, rows(plane * width, skip)],
+                landed_ref.at[:, rows(0, skip)],
                 land_send.at[1, j],
                 land_recv.at[0],
                 j * PLANE + role,
@@ -609,34 +816,36 @@
         return carry
 
     lax.fori_loop(0, planes, climb, 0)
+
+    with jax.named_scope("relay"):
+        descend(relay)
+
     settle = pltpu.make_async_copy(
         kv.at[plane, :, rows(BACK, width)],
         landed_ref.at[:, rows(plane * width, width)],
         load_sem.at[0],
     )
     settle.start()
-    await_(qs.at[:, place], local_sem.at[1])
-
-    factor = HEAD_DIM ** (-0.5) * math.log2(math.e)
-    nt = (((1,), (1,)), ((), ()))
-    span = (BACK + here) * BLOCK
-
-    def attend(j, i):
+
+    def attend(j, i, variant):
         window = pl.ds(i * tokens, span)
-        q = qs[j, pl.ds(i * tokens, tokens), :]
-        s = lax.dot_general(q, kv[j, 0, window, :], nt, preferred_element_type=jnp.float32)
-        s = s + bias[i]
-        peak = jnp.max(s, axis=1, keepdims=True)
-        w = jnp.exp2((s - peak) * factor)
-        total = jnp.sum(w, axis=1, keepdims=True)
-        mixed = jnp.dot(
-            w.astype(jnp.bfloat16), kv[j, 1, window, :], preferred_element_type=jnp.float32
-        )
+        return soften(
+            qs[j, pl.ds(i * tokens, tokens), :],
+            kv[j, 0, window, :],
+            kv[j, 1, window, :],
+            bias[variant, i],
+        )
+
+    def finish(j, i, mixed, total):
         real = jnp.concatenate(
             [column < valids[BACK + i * here + b] for b in range(here)], axis=0
         )
         mixed_ref[j, i] = jnp.where(real, mixed / total, 0.0).astype(mixed_ref.dtype)
 
+    def simple(j, i):
+        mixed, _, total = attend(j, i, 0)
+        finish(j, i, mixed, total)
+
     def give(j, i):
         target = out_ref.at[:, cols(j * PLANE + role)]
 
@@ -648,93 +857,150 @@
         def _():
             remote(mixed_ref.at[j, i], target, out_send.at[0], out_recv.at[0], base + i)
 
-    def one_head(t, carry):
-        j = planes - 1 - t
-        for k in range(PLANE - 1):
-            await_(qs.at[j, rows(peers[k] * here, here)], q_recv.at[k, j])
-        attend(j, PLANE - 1)
-
-        @pl.when(t > 0)
-        def _():
-            give(jnp.minimum(j + 1, planes - 1), 0)
-
-        @pl.when(late)
-        def _():
-            for rho in range(PLANE):
-                count = min(here, (rho + 1) * here - skip)
-                if count > 0:
-                    await_(
-                        kv.at[j, :, rows(max(rho * here - skip, 0), count)],
-                        halo_recv.at[j, rho],
-                    )
-
-        @pl.when(late & (j > plane))
-        def _():
-            remote(
-                kv.at[j, :, rows(0, BACK)],
-                landed_ref.at[:, rows(jnp.maximum(plane * width - BACK, 0), BACK)],
-                land_send.at[2, j],
-                land_recv.at[0],
-                j * PLANE + role,
-            )
-
-        for i in range(PLANE - 2, -1, -1):
-            attend(j, i)
-            give(j, i + 1)
+    top = PLANE - 1
+
+    def own_blocks(t, carry):
+        j = last - t
+        with jax.named_scope("wait_q"):
+
+            @pl.when(jnp.logical_not(helped(j)))
+            def _():
+                await_q(j)
+
+        with jax.named_scope("top"):
+            simple(j, top)
+
+            @pl.when(t > 0)
+            def _():
+                give(jnp.minimum(j + 1, last), top)
+
         return carry
 
-    lax.fori_loop(0, planes, one_head, 0)
+    lax.fori_loop(0, planes, own_blocks, 0)
+
+    def reach_back(j):
+        with jax.named_scope("wait_halo"):
+
+            @pl.when(late & (j <= plane))
+            def _():
+                await_halo(j)
+
+        with jax.named_scope("units"):
+            for i in range(top - 1, -1, -1):
+                simple(j, i)
+                if i == top - 1:
+
+                    @pl.when(j == last)
+                    def _():
+                        give(0, top)
+
+                    @pl.when(j < last)
+                    def _():
+                        give(jnp.minimum(j + 1, last), 0)
+
+                else:
+                    give(j, i + 1)
+
+    descend(when_helped(reach_back, False))
 
     settled = pltpu.make_async_copy(
-        kv.at[plane, :, rows(0, BACK)],
-        landed_ref.at[:, rows(jnp.maximum(plane * width - BACK, 0), BACK)],
-        load_sem.at[1],
+        kv.at[plane, :, rows(0, BACK)], landed_ref.at[:, below], load_sem.at[1]
     )
 
     @pl.when(late)
     def _():
         settled.start()
 
-    give(0, 0)
-
-    others = features // PLANE * (PLANE - 1)
-    await_(own.at[:, :, pl.ds(0, others)], kv_send.at[0])
-    await_(q_ref.at[:, pl.ds(0, others)], q_send.at[0])
-    await_(q_ref.at[:, pl.ds(0, features // PLANE)], local_sem.at[2])
-
-    @pl.when(more)
-    def _():
-        await_(kv.at[:, :, rows(0, BACK)], halo_send.at[0])
-
-    def drain(j, carry):
-        @pl.when(j < plane)
-        def _():
-            await_(kv.at[j, :, rows(BACK, width)], land_send.at[0, j])
-
-        @pl.when(j > plane)
-        def _():
-            await_(kv.at[j, :, rows(BACK, skip)], land_send.at[1, j])
-
-        @pl.when(late & (j > plane))
-        def _():
-            await_(kv.at[j, :, rows(0, BACK)], land_send.at[2, j])
-
-        return carry
-
-    lax.fori_loop(0, planes, drain, 0)
-    settle.wait()
-
-    @pl.when(late)
-    def _():
-        settled.wait()
-        await_(landed_ref.at[:, rows(0, (planes - 1) * width - BACK)], land_recv.at[0])
-
-    @pl.when(plane == 0)
-    def _():
-        await_(landed_ref.at[:, rows(0, (planes - 1) * width)], land_recv.at[0])
-
-    await_(q_ref.at[:, pl.ds(0, others)], out_send.at[0])
-    await_(q_ref.at[:, pl.ds(0, others)], out_recv.at[0])
+    for j in range(planes):
+        first = jnp.logical_not(helped(j))
+
+        @pl.when(first & helped(j - 1) if j else first)
+        def _():
+            give(j, 0)
+
+    def merge(j):
+        with jax.named_scope("wait_part"):
+            await_(part_in.at[j], up_recv.at[0, j])
+            await_(size_in.at[j], up_recv.at[1, j])
+        with jax.named_scope("merge"):
+            for i in range(top - 1, -1, -1):
+                mixed, peak, total = attend(j, i, 1)
+                mixed = [mixed[b * BLOCK : (b + 1) * BLOCK] for b in range(here)]
+                total = [
+                    jnp.broadcast_to(total[b * BLOCK : (b + 1) * BLOCK], (BLOCK, BLOCK))
+                    for b in range(here)
+                ]
+                for b in range(here):
+                    g = i * here + b
+                    if g < BACK:
+                        size = jnp.broadcast_to(size_in[j, g, :1], (BLOCK, BLOCK)).T
+                        mark = peak[b * BLOCK : (b + 1) * BLOCK]
+                        high = jnp.maximum(mark, size)
+                        mine_share = jnp.exp2(mark - high)
+                        their_share = jnp.exp2(size - high)
+                        theirs = part_in[j, g * BLOCK : (g + 1) * BLOCK, :]
+                        mixed[b] = mixed[b] * mine_share + theirs.astype(jnp.float32) * their_share
+                        total[b] = total[b] * mine_share + their_share
+                finish(
+                    j, i, jnp.concatenate(mixed, axis=0), jnp.concatenate(total, axis=0)
+                )
+                if i < top - 1:
+                    give(j, i + 1)
+        give(j, 0)
+
+    for h in helpable:
+
+        @pl.when(helped(h))
+        def _():
+            merge(h)
+
+    with jax.named_scope("drain"):
+        others = features // PLANE * (PLANE - 1)
+        await_(own.at[:, :, pl.ds(0, others)], kv_send.at[0])
+        await_(q_ref.at[:, pl.ds(0, others)], q_send.at[0])
+        await_(q_ref.at[:, pl.ds(0, features // PLANE)], local_sem.at[2])
+
+        def drain(j):
+            @pl.when(more & jnp.logical_not(helps(j)))
+            def _():
+                await_(kv.at[j, :, rows(0, BACK)], halo_send.at[j])
+
+            @pl.when(helps(j))
+            def _():
+                await_(part_out.at[j], up_send.at[0, j])
+                await_(size_out.at[j], up_send.at[1, j])
+
+            @pl.when(helped(j))
+            def _():
+                await_(lower_q.at[j], down_send.at[j])
+
+            @pl.when(j < plane)
+            def _():
+                await_(kv.at[j, :, rows(BACK, width)], land_send.at[0, j])
+
+            @pl.when(j > plane)
+            def _():
+                await_(kv.at[j, :, rows(BACK, skip)], land_send.at[1, j])
+
+            @pl.when(late & (j > plane))
+            def _():
+                await_(kv.at[j, :, rows(0, BACK)], land_send.at[2, j])
+
+        each(drain)
+        settle.wait()
+        await_(q_ref.at[:, pl.ds(0, others)], out_send.at[0])
+        await_(q_ref.at[:, pl.ds(0, others)], out_recv.at[0])
+
+    with jax.named_scope("land"):
+
+        @pl.when(late)
+        def _():
+            settled.wait()
+            await_(landed_ref.at[:, rows(0, (planes - 1) * width - BACK)], land_recv.at[0])
+
+        @pl.when(plane == 0)
+        def _():
+            await_(landed_ref.at[:, rows(0, (planes - 1) * width)], land_recv.at[0])
 
 
 def wide_exchange(n, queries, keys, values, block_counts, last_tokens, pack_order):
@@ -784,6 +1050,7 @@
     anywhere = pl.BlockSpec(memory_space=pl.ANY)
     dma = pltpu.SemaphoreType.DMA
     planes = n // PLANE
+    reach = BACK * BLOCK
     if splits == 1 and here == 2 and planes > 1:
         attended, landed = pl.pallas_call(
             functools.partial(handoff, n),
@@ -799,19 +1066,29 @@
                 pltpu.VMEM((planes, 2, (BACK + PLANE * here) * BLOCK, HEAD_DIM), kind),
                 pltpu.VMEM((planes, PLANE * tokens, HEAD_DIM), kind),
                 pltpu.VMEM((planes, PLANE, tokens, HEAD_DIM), kind),
-                pltpu.VMEM((PLANE, tokens, (BACK + here) * BLOCK), jnp.float32),
+                pltpu.VMEM((2, PLANE, tokens, (BACK + here) * BLOCK), jnp.float32),
+                pltpu.VMEM((planes, reach, HEAD_DIM), kind),
+                pltpu.VMEM((reach, reach), jnp.float32),
+                pltpu.VMEM((planes, reach, HEAD_DIM), kind),
+                pltpu.VMEM((planes, reach, HEAD_DIM), kind),
+                pltpu.VMEM((planes, BACK, 8, BLOCK), jnp.float32),
+                pltpu.VMEM((planes, BACK, 8, BLOCK), jnp.float32),
                 dma((3,)),
                 dma((3,)),
                 dma((1,)),
                 dma((PLANE - 1, planes)),
                 dma((1,)),
                 dma((PLANE - 1, planes)),
-                dma((1,)),
+                dma((planes,)),
                 dma((planes, PLANE)),
                 dma((3, planes)),
                 dma((1,)),
                 dma((1,)),
                 dma((1,)),
+                dma((planes,)),
+                dma((planes,)),
+                dma((2, planes)),
+                dma((2, planes)),
             ],
             compiler_params=pltpu.CompilerParams(
                 collective_id=0, has_side_effects=True, vmem_limit_bytes=60 * 1024 * 1024

time: 68.8 us -> 63.4 us (0.922)
  Pallas kernels: 68 us -> 62.2 us
    pallas_call x1, Pallas kernels: 64.1 us -> 58.3 us  [local(): pl.pallas_call(functools.partial(handoff, n), out_shape=(jax.ShapeDtypeSt...]
where the time goes in v1:
time: 63.4 us; the launch traced here: 62.8 us
  Pallas kernels  62.2 us (98%)
  between operations  0.64 us (1%)
    pallas_call x1, Pallas kernels, local(): pl.pallas_call(functools.partial(handoff, n), out_shape=(jax.ShapeDtypeSt...  58.3 us
    pallas_call x1, Pallas kernels, local(): pl.pallas_call(reorder, out_shape=(jax.ShapeDtypeStruct((tokens, features...  3.9 us

profile of v1, /device:TPU:18, one launch (start us, length us, event | category | flops | bytes accessed | tf_op | source)
XLA Modules:
  0.0 62.8 jit_solution(15453250122383657465)
XLA Ops:
  0.6 58.3 %shard_map.94 = (bf16[256,2048]{1,0:T(8,128)(2,1)}, bf16[2,4096,128]{2,1,0:T(8,128)(2,1)}) custom-call(s32[8]{0:T(128)} %counts_ref.3, s32[16]{0:T(128)} %tails_ref.1, s32[16]{0:T(128)} %order_ref.3, bf16[256,2048]{1,0:T(8,128)(2,1)} %q_hbm.1, bf16[256,2048]{1,0:T(8,128)(2,1)} %k_hbm.1, bf16[256,2048]{1,0:T(8,128)(2,1)} %v_hbm.1), custom_call_target="tpu_custom_call" | custom-call | tf_op jit(solution)/shard_map/pallas_call | solution.py:1055
  58.9 3.9 %shard_map.95 = (bf16[256,2048]{1,0:T(8,128)(2,1)}, bf16[1,32,128,128]{3,2,1,0:T(8,128)(2,1)}, bf16[1,32,128,128]{3,2,1,0:T(8,128)(2,1)}) custom-call(s32[8]{0:T(128)} %counts_ref.3, s32[16]{0:T(128)} %order_ref.3, s32[8]{0:T(128)} %slot_ref.1, bf16[2,4096,128]{2,1,0:T(8,128)(2,1)} %get-tuple-element.5.landed_ref, bf16[256,2048]{1,0:T(8,128)(2,1)} %get-tuple-element.6.mixed_ref), custom_call_target="tpu_custom_call" | custom-call | tf_op jit(solution)/shard_map/pallas_call | solution.py:1102

commit v2 on v1

--- a/solution.py
+++ b/solution.py
@@ -304,7 +304,76 @@
     pltpu.make_async_copy(ref, ref, cache_sem.at[1]).wait()
 
 
+def decode_places(counts_ref, order_ref, slot_ref, who, base, put):
+    pairs = counts_ref.shape[0]
+    prompts = order_ref.shape[0]
+
+    def invert(p, carry):
+        who[slot_ref[p]] = p
+        return carry
+
+    lax.fori_loop(0, pairs, invert, 0)
+
+    def lay(s, first):
+        p = who[s]
+        base[p] = first
+        return first + counts_ref[p] + 1
+
+    lax.fori_loop(0, pairs, lay, jnp.int32(0))
+
+    def fetch(i, first):
+        prompt = order_ref[i]
+        pair = lax.rem(prompt, pairs)
+        null = prompt >= pairs
+        counted = counts_ref[pair]
+        size = jnp.where(null, 1, counted)
+        target = base[pair] + jnp.where(null, counted, 0)
+
+        def one(w, carry):
+            put(first + w, target + w)
+            return carry
+
+        lax.fori_loop(0, size, one, 0)
+        return first + size
+
+    lax.fori_loop(0, prompts, fetch, jnp.int32(0))
+
+
 def reorder(
+    counts_ref,
+    order_ref,
+    slot_ref,
+    landed_ref,
+    keys_ref,
+    values_ref,
+    staged,
+    who,
+    base,
+    in_sem,
+    out_sem,
+):
+    part = staged.shape[2]
+
+    def put(source, target):
+        for kv in range(2):
+            pltpu.make_async_copy(
+                landed_ref.at[kv, pl.ds(source * part, part)],
+                staged.at[kv, target],
+                in_sem.at[kv],
+            ).start()
+
+    decode_places(counts_ref, order_ref, slot_ref, who, base, put)
+    outs = []
+    for kv, ref in enumerate((keys_ref, values_ref)):
+        pltpu.make_async_copy(staged.at[kv], staged.at[kv], in_sem.at[kv]).wait()
+        copy = pltpu.make_async_copy(staged.at[kv], ref.at[0], out_sem.at[kv])
+        copy.start()
+        outs.append(copy)
+    for copy in outs:
+        copy.wait()
+
+
+def publish(
     counts_ref,
     order_ref,
     slot_ref,
@@ -313,63 +382,25 @@
     attended_ref,
     keys_ref,
     values_ref,
-    staged,
-    passed,
     who,
     base,
-    in_sem,
     out_sem,
 ):
-    enter = pltpu.make_async_copy(mixed_ref, passed, in_sem.at[2])
-    enter.start()
-    pairs = counts_ref.shape[0]
-    prompts = order_ref.shape[0]
-    blocks, part = staged.shape[1:3]
-
-    def invert(p, carry):
-        who[slot_ref[p]] = p
-        return carry
-
-    lax.fori_loop(0, pairs, invert, 0)
-
-    def lay(s, first):
-        p = who[s]
-        base[p] = first
-        return first + counts_ref[p] + 1
-
-    lax.fori_loop(0, pairs, lay, jnp.int32(0))
-
-    def fetch(i, first):
-        prompt = order_ref[i]
-        pair = lax.rem(prompt, pairs)
-        null = prompt >= pairs
-        counted = counts_ref[pair]
-        size = jnp.where(null, 1, counted)
-        target = base[pair] + jnp.where(null, counted, 0)
-
-        def one(w, carry):
-            for kv in range(2):
-                pltpu.make_async_copy(
-                    landed_ref.at[kv, pl.ds((first + w) * part, part)],
-                    staged.at[kv, target + w],
-                    in_sem.at[kv],
-                ).start()
-            return carry
-
-        lax.fori_loop(0, size, one, 0)
-        return first + size
-
-    lax.fori_loop(0, prompts, fetch, jnp.int32(0))
-    enter.wait()
-    outs = [pltpu.make_async_copy(passed, attended_ref, out_sem.at[2])]
-    outs[0].start()
-    for kv, ref in enumerate((keys_ref, values_ref)):
-        pltpu.make_async_copy(staged.at[kv], staged.at[kv], in_sem.at[kv]).wait()
-        copy = pltpu.make_async_copy(staged.at[kv], ref.at[0], out_sem.at[kv])
-        copy.start()
-        outs.append(copy)
-    for copy in outs:
-        copy.wait()
+    leave = pltpu.make_async_copy(mixed_ref, attended_ref, out_sem.at[2])
+    leave.start()
+    refs = (keys_ref, values_ref)
+    part = keys_ref.shape[2]
+
+    def put(source, target):
+        for kv, ref in enumerate(refs):
+            pltpu.make_async_copy(
+                landed_ref.at[kv, pl.ds(source * part, part)], ref.at[0, target], out_sem.at[kv]
+            ).start()
+
+    decode_places(counts_ref, order_ref, slot_ref, who, base, put)
+    leave.wait()
+    for kv, ref in enumerate(refs):
+        pltpu.make_async_copy(ref.at[0], ref.at[0], out_sem.at[kv]).wait()
 
 
 def handoff(
@@ -492,20 +523,6 @@
             ((k_hbm, own.at[0]), (v_hbm, own.at[1]), (q_hbm, q_ref))
         )
     ]
-    for load in loads:
-        load.start()
-    for j in range(planes):
-        here_cols = cols(j * PLANE + role)
-        for i, src in enumerate((k_hbm, v_hbm)):
-            pltpu.make_async_copy(
-                src.at[:, here_cols], kv.at[j, i, mine], local_sem.at[0]
-            ).start()
-    for j in range(planes):
-        here_cols = cols(j * PLANE + role)
-        pltpu.make_async_copy(
-            q_hbm.at[:, here_cols], qs.at[j, place], local_sem.at[1]
-        ).start()
-
     barrier = pltpu.get_barrier_semaphore()
     for peer in peers:
         pl.semaphore_signal(
@@ -521,6 +538,19 @@
             device_id={"seq": lax.rem(me + step * PLANE, n)},
             device_id_type=pl.DeviceIdType.MESH,
         )
+    for j in range(planes):
+        here_cols = cols(j * PLANE + role)
+        for i, src in enumerate((k_hbm, v_hbm)):
+            pltpu.make_async_copy(
+                src.at[:, here_cols], kv.at[j, i, mine], local_sem.at[0]
+            ).start()
+    for load in loads:
+        load.start()
+    for j in range(planes):
+        here_cols = cols(j * PLANE + role)
+        pltpu.make_async_copy(
+            q_hbm.at[:, here_cols], qs.at[j, place], local_sem.at[1]
+        ).start()
 
     for j in range(planes):
 
@@ -528,11 +558,6 @@
         def _():
             for i in range(2):
                 kv[j, i, :reach, :] = jnp.zeros((reach, HEAD_DIM), kv.dtype)
-
-    with jax.named_scope("enter"):
-        for load in loads:
-            load.wait()
-        pl.semaphore_wait(barrier, PLANE - 1 + planes - 1)
 
     def share(j):
         for k in (1, 2, 0):
@@ -569,10 +594,6 @@
 
         lax.fori_loop(0, planes, step, 0)
 
-    each(when_helped(share_q, True))
-    each(share)
-    descend(when_helped(share_q, False))
-
     def forward(j, rho):
         first = BACK + rho * here
         low = rho * here < skip
@@ -649,8 +670,19 @@
 
         return body
 
-    await_(kv.at[:, :, mine], local_sem.at[0])
-    each(start_mine)
+    with jax.named_scope("enter_local"):
+        await_(kv.at[:, :, mine], local_sem.at[0])
+    with jax.named_scope("enter_barrier"):
+        pl.semaphore_wait(barrier, PLANE - 1 + planes - 1)
+    with jax.named_scope("start_mine"):
+        each(start_mine)
+    with jax.named_scope("enter_loads"):
+        for load in loads:
+            load.wait()
+    with jax.named_scope("share"):
+        each(when_helped(share_q, True))
+        each(share)
+        descend(when_helped(share_q, False))
 
     with jax.named_scope("take_core"):
         each(start_core(False))
@@ -1051,12 +1083,13 @@
     dma = pltpu.SemaphoreType.DMA
     planes = n // PLANE
     reach = BACK * BLOCK
+    cache = jax.ShapeDtypeStruct((1, blocks, part, HEAD_DIM), kind)
     if splits == 1 and here == 2 and planes > 1:
         attended, landed = pl.pallas_call(
             functools.partial(handoff, n),
             out_shape=(
-                jax.ShapeDtypeStruct((tokens, features), kind),
-                jax.ShapeDtypeStruct((2, blocks * part, HEAD_DIM), kind),
+                pltpu.VMEM((tokens, features), kind),
+                pltpu.VMEM((2, blocks * part, HEAD_DIM), kind),
             ),
             in_specs=[smem] * 3 + [anywhere] * 3,
             out_specs=(anywhere, anywhere),
@@ -1094,25 +1127,39 @@
                 collective_id=0, has_side_effects=True, vmem_limit_bytes=60 * 1024 * 1024
             ),
         )(block_counts, last_tokens, pack_order, queries, keys, values)
-    else:
-        attended, landed = wide_exchange(
-            n, queries, keys, values, block_counts, last_tokens, pack_order
-        )
-    cache = jax.ShapeDtypeStruct((1, blocks, part, HEAD_DIM), kind)
-    attended, cache_keys, cache_values = pl.pallas_call(
+        return pl.pallas_call(
+            publish,
+            out_shape=(jax.ShapeDtypeStruct((tokens, features), kind), cache, cache),
+            in_specs=[smem] * 3 + [anywhere] * 2,
+            out_specs=(anywhere,) * 3,
+            scratch_shapes=[
+                pltpu.SMEM(block_counts.shape, jnp.int32),
+                pltpu.SMEM(block_counts.shape, jnp.int32),
+                dma((3,)),
+            ],
+        )(
+            block_counts,
+            pack_order,
+            decode_slot,
+            pltpu.with_memory_space_constraint(landed, pltpu.VMEM),
+            pltpu.with_memory_space_constraint(attended, pltpu.VMEM),
+        )
+    attended, landed = wide_exchange(
+        n, queries, keys, values, block_counts, last_tokens, pack_order
+    )
+    cache_keys, cache_values = pl.pallas_call(
         reorder,
-        out_shape=(jax.ShapeDtypeStruct((tokens, features), kind), cache, cache),
-        in_specs=[smem] * 3 + [anywhere] * 2,
-        out_specs=(anywhere,) * 3,
+        out_shape=(cache, cache),
+        in_specs=[smem] * 3 + [anywhere],
+        out_specs=(anywhere, anywhere),
         scratch_shapes=[
             pltpu.VMEM((2, blocks, part, HEAD_DIM), kind),
-            pltpu.VMEM((tokens, features), kind),
             pltpu.SMEM(block_counts.shape, jnp.int32),
             pltpu.SMEM(block_counts.shape, jnp.int32),
-            dma((3,)),
-            dma((3,)),
+            dma((2,)),
+            dma((2,)),
         ],
-    )(block_counts, pack_order, decode_slot, landed, attended)
+    )(block_counts, pack_order, decode_slot, landed)
     return attended, cache_keys, cache_values
 
 

time: 63.4 us -> 61.7 us (0.973)
  Pallas kernels: 62.2 us -> 60.4 us
    pallas_call x2, Pallas kernels: 62.2 us -> 60.4 us  [the longest x1 58 us: local(): pl.pallas_call(functools.partial(handoff, n), out_shape=(pltpu.VMEM((toke...]
where the time goes in v2:
time: 61.7 us; the launch traced here: 61 us
  Pallas kernels  60.4 us (98%)
  between operations  0.64 us (1%)
    pallas_call x1, Pallas kernels, local(): pl.pallas_call(functools.partial(handoff, n), out_shape=(pltpu.VMEM((toke...  58 us
    pallas_call x1, Pallas kernels, local(): pl.pallas_call(publish, out_shape=(jax.ShapeDtypeStruct((tokens, features...  2.33 us

profile of v2, /device:TPU:18, one launch (start us, length us, event | category | flops | bytes accessed | tf_op | source)
XLA Modules:
  0.0 61.0 jit_solution(9014842166649027818)
XLA Ops:
  0.6 58.0 %shard_map.94 = (bf16[256,2048]{1,0:T(8,128)(2,1)S(1)}, bf16[2,4096,128]{2,1,0:T(8,128)(2,1)S(1)}) custom-call(s32[8]{0:T(128)} %counts_ref.3, s32[16]{0:T(128)} %tails_ref.1, s32[16]{0:T(128)} %order_ref.3, bf16[256,2048]{1,0:T(8,128)(2,1)} %q_hbm.1, bf16[256,2048]{1,0:T(8,128)(2,1)} %k_hbm.1, bf16[256,2048]{1,0:T(8,128)(2,1)} %v_hbm.1), custom_call_target="tpu_custom_call" | custom-call | tf_op jit(solution)/shard_map/pallas_call | solution.py:1088
  58.7 2.3 %shard_map.95 = (bf16[256,2048]{1,0:T(8,128)(2,1)}, bf16[1,32,128,128]{3,2,1,0:T(8,128)(2,1)}, bf16[1,32,128,128]{3,2,1,0:T(8,128)(2,1)}) custom-call(s32[8]{0:T(128)} %counts_ref.3, s32[16]{0:T(128)} %order_ref.3, s32[8]{0:T(128)} %slot_ref.1, bf16[2,4096,128]{2,1,0:T(8,128)(2,1)S(1)} %get-tuple-element.5.landed_ref, ...), custom_call_target="tpu_custom_call" | custom-call | tf_op jit(solution)/shard_map/pallas_call | solution.py:1130

commit v3 on v2

--- a/solution.py
+++ b/solution.py
@@ -373,31 +373,22 @@
         copy.wait()
 
 
-def publish(
-    counts_ref,
-    order_ref,
-    slot_ref,
-    landed_ref,
-    mixed_ref,
-    attended_ref,
-    keys_ref,
-    values_ref,
-    who,
-    base,
-    out_sem,
-):
+def publish(places_ref, landed_ref, mixed_ref, attended_ref, keys_ref, values_ref, out_sem):
     leave = pltpu.make_async_copy(mixed_ref, attended_ref, out_sem.at[2])
     leave.start()
     refs = (keys_ref, values_ref)
     part = keys_ref.shape[2]
 
-    def put(source, target):
+    def put(b, carry):
         for kv, ref in enumerate(refs):
             pltpu.make_async_copy(
-                landed_ref.at[kv, pl.ds(source * part, part)], ref.at[0, target], out_sem.at[kv]
+                landed_ref.at[kv, pl.ds(pl.multiple_of(b * part, part), part)],
+                ref.at[0, places_ref[b]],
+                out_sem.at[kv],
             ).start()
-
-    decode_places(counts_ref, order_ref, slot_ref, who, base, put)
+        return carry
+
+    lax.fori_loop(0, places_ref.shape[0], put, 0)
     leave.wait()
     for kv, ref in enumerate(refs):
         pltpu.make_async_copy(ref.at[0], ref.at[0], out_sem.at[kv]).wait()
@@ -405,14 +396,20 @@
 
 def handoff(
     n,
-    counts_ref,
-    tails_ref,
-    order_ref,
+    counts_hbm,
+    tails_hbm,
+    order_hbm,
+    slot_hbm,
     q_hbm,
     k_hbm,
     v_hbm,
     out_ref,
     landed_ref,
+    places_ref,
+    counts_ref,
+    tails_ref,
+    order_ref,
+    slot_ref,
     q_ref,
     own,
     kv,
@@ -425,6 +422,7 @@
     part_in,
     size_out,
     size_in,
+    small_sem,
     load_sem,
     local_sem,
     kv_send,
@@ -546,6 +544,19 @@
             ).start()
     for load in loads:
         load.start()
+    smalls = [
+        pltpu.make_async_copy(src, dst, small_sem.at[i])
+        for i, (src, dst) in enumerate(
+            (
+                (counts_hbm, counts_ref),
+                (tails_hbm, tails_ref),
+                (order_hbm, order_ref),
+                (slot_hbm, slot_ref),
+            )
+        )
+    ]
+    for small in smalls:
+        small.start()
     for j in range(planes):
         here_cols = cols(j * PLANE + role)
         pltpu.make_async_copy(
@@ -660,7 +671,9 @@
 
     def start_core(truth):
         def body(j):
-            @pl.when(helped(j) if truth else jnp.logical_not(helped(j)))
+            later = helped(j) & (j > 0)
+
+            @pl.when(later if truth else jnp.logical_not(later))
             def _():
                 take(0, j)
 
@@ -688,6 +701,8 @@
         each(start_core(False))
 
     with jax.named_scope("tables"):
+        for small in smalls:
+            small.wait()
         docs, valids = window_tables(
             counts_ref, tails_ref, order_ref, plane * width - BACK, BACK + width + BACK
         )
@@ -765,6 +780,42 @@
                 land_recv.at[0],
                 j * PLANE + role,
             )
+
+    def map_places():
+        pairs = counts_ref.shape[0]
+        blocks = places_ref.shape[0]
+
+        def empty(b, carry):
+            places_ref[b] = 0
+            return carry
+
+        lax.fori_loop(0, blocks, empty, 0)
+
+        def fill(i, first):
+            prompt = order_ref[i]
+            pair = lax.rem(prompt, pairs)
+            null = prompt >= pairs
+            counted = counts_ref[pair]
+            end = first + jnp.where(null, 1, counted)
+            slot = slot_ref[pair]
+
+            def earlier(p, total):
+                return total + jnp.where(slot_ref[p] < slot, counts_ref[p] + 1, 0)
+
+            target = lax.fori_loop(0, pairs, earlier, jnp.where(null, counted, 0)) - first
+
+            def mark(b, carry):
+                inside = (first <= b) & (b < end)
+                places_ref[b] = jnp.where(inside, target + b, places_ref[b])
+                return carry
+
+            lax.fori_loop(0, blocks, mark, 0)
+            return end
+
+        lax.fori_loop(0, order_ref.shape[0], fill, jnp.int32(0))
+
+    with jax.named_scope("map_places"):
+        map_places()
 
     factor = HEAD_DIM ** (-0.5) * math.log2(math.e)
     nt = (((1,), (1,)), ((), ()))
@@ -1085,15 +1136,20 @@
     reach = BACK * BLOCK
     cache = jax.ShapeDtypeStruct((1, blocks, part, HEAD_DIM), kind)
     if splits == 1 and here == 2 and planes > 1:
-        attended, landed = pl.pallas_call(
+        attended, landed, places = pl.pallas_call(
             functools.partial(handoff, n),
             out_shape=(
                 pltpu.VMEM((tokens, features), kind),
                 pltpu.VMEM((2, blocks * part, HEAD_DIM), kind),
+                pltpu.SMEM((blocks,), jnp.int32),
             ),
-            in_specs=[smem] * 3 + [anywhere] * 3,
-            out_specs=(anywhere, anywhere),
+            in_specs=[anywhere] * 7,
+            out_specs=(anywhere, anywhere, smem),
             scratch_shapes=[
+                pltpu.SMEM(block_counts.shape, jnp.int32),
+                pltpu.SMEM(last_tokens.shape, jnp.int32),
+                pltpu.SMEM(pack_order.shape, jnp.int32),
+                pltpu.SMEM(decode_slot.shape, jnp.int32),
                 pltpu.VMEM((tokens, features), kind),
                 pltpu.VMEM((2, tokens, features), kind),
                 pltpu.VMEM((planes, 2, (BACK + PLANE * here) * BLOCK, HEAD_DIM), kind),
@@ -1106,6 +1162,7 @@
                 pltpu.VMEM((planes, reach, HEAD_DIM), kind),
                 pltpu.VMEM((planes, BACK, 8, BLOCK), jnp.float32),
                 pltpu.VMEM((planes, BACK, 8, BLOCK), jnp.float32),
+                dma((4,)),
                 dma((3,)),
                 dma((3,)),
                 dma((1,)),
@@ -1126,21 +1183,15 @@
             compiler_params=pltpu.CompilerParams(
                 collective_id=0, has_side_effects=True, vmem_limit_bytes=60 * 1024 * 1024
             ),
-        )(block_counts, last_tokens, pack_order, queries, keys, values)
+        )(block_counts, last_tokens, pack_order, decode_slot, queries, keys, values)
         return pl.pallas_call(
             publish,
             out_shape=(jax.ShapeDtypeStruct((tokens, features), kind), cache, cache),
-            in_specs=[smem] * 3 + [anywhere] * 2,
+            in_specs=[smem] + [anywhere] * 2,
             out_specs=(anywhere,) * 3,
-            scratch_shapes=[
-                pltpu.SMEM(block_counts.shape, jnp.int32),
-                pltpu.SMEM(block_counts.shape, jnp.int32),
-                dma((3,)),
-            ],
+            scratch_shapes=[dma((3,))],
         )(
-            block_counts,
-            pack_order,
-            decode_slot,
+            pltpu.with_memory_space_constraint(places, pltpu.SMEM),
             pltpu.with_memory_space_constraint(landed, pltpu.VMEM),
             pltpu.with_memory_space_constraint(attended, pltpu.VMEM),
         )

time: 61.7 us -> 60.3 us (0.977)
  Pallas kernels: 60.4 us -> 59 us
    pallas_call x1, Pallas kernels: 2.33 us -> 1.65 us  [local(): pl.pallas_call(publish, out_shape=(jax.ShapeDtypeStruct((tokens, features...]
    pallas_call x1, Pallas kernels: 58 us -> 57.4 us  [local(): pl.pallas_call(functools.partial(handoff, n), out_shape=(pltpu.VMEM((toke...]
where the time goes in v3:
time: 60.3 us; the launch traced here: 59.7 us
  Pallas kernels  59 us (98%)
  between operations  0.64 us (1%)
    pallas_call x1, Pallas kernels, local(): pl.pallas_call(functools.partial(handoff, n), out_shape=(pltpu.VMEM((toke...  57.4 us
    pallas_call x1, Pallas kernels, local(): pl.pallas_call(publish, out_shape=(jax.ShapeDtypeStruct((tokens, features...  1.65 us

profile of v3, /device:TPU:18, one launch (start us, length us, event | category | flops | bytes accessed | tf_op | source)
XLA Modules:
  0.0 59.7 jit_solution(1152002981092135191)
XLA Ops:
  0.6 57.4 %shard_map.94 = (bf16[256,2048]{1,0:T(8,128)(2,1)S(1)}, bf16[2,4096,128]{2,1,0:T(8,128)(2,1)S(1)}, s32[32]{0:T(128)S(4)}) custom-call(s32[8]{0:T(128)} %counts_hbm.1, s32[16]{0:T(128)} %tails_hbm.1, s32[16]{0:T(128)} %order_hbm.1, s32[8]{0:T(128)} %slot_hbm.1, bf16[256,2048]{1,0:T(8,128)(2,1)} %q_hbm.1, bf16[256,2048]{1,0:T(8,128)(2,1)} %k_hbm.1, ...), custom_call_target="tpu_custom_call" | custom-call | tf_op jit(solution)/shard_map/pallas_call | solution.py:1139
  58.0 1.7 %shard_map.95 = (bf16[256,2048]{1,0:T(8,128)(2,1)}, bf16[1,32,128,128]{3,2,1,0:T(8,128)(2,1)}, bf16[1,32,128,128]{3,2,1,0:T(8,128)(2,1)}) custom-call(s32[32]{0:T(128)S(4)} %get-tuple-element.6.places_ref, bf16[2,4096,128]{2,1,0:T(8,128)(2,1)S(1)} %get-tuple-element.7.landed_ref, bf16[256,2048]{1,0:T(8,128)(2,1)S(1)} %get-tuple-element.8.mixed_ref), custom_call_target="tpu_custom_call" | custom-call | tf_op jit(solution)/shard_map/pallas_call | solution.py:1187

commit v4 on v3

--- a/solution.py
+++ b/solution.py
@@ -18,6 +18,8 @@
 CHUNKS = 4
 RELAY = BACK
 ROUND = 2
+NEAR = 2
+FEW = MAXB - NEAR - 1
 
 
 def window_tables(counts_ref, tails_ref, order_ref, first, width):
@@ -418,8 +420,7 @@
     bias,
     lower_q,
     lower_bias,
-    part_out,
-    part_in,
+    slot_out,
     size_out,
     size_in,
     small_sem,
@@ -449,6 +450,8 @@
     width = PLANE * here
     skip = width - BACK
     reach = BACK * BLOCK
+    few_rows = FEW * BLOCK
+    far_rows = (BACK - NEAR) * BLOCK
     peers = (role + 1 - 2 * lax.rem(role, 2), lax.rem(role + 2, PLANE), PLANE - 1 - role)
     more = plane < planes - 1
     late = plane > 0
@@ -457,7 +460,7 @@
     orders = []
     for p in range(planes):
         above = list(range(last, p, -1))
-        helping = [j for j in range(p + 1) if j + p < last and 2 * p >= planes - 2]
+        helping = [j for j in range(p + 1) if 2 * j < planes and 2 * p >= planes - 2]
         rest = [j for j in range(p, -1, -1) if j not in helping]
         if p == last:
             above, helping, rest = [last - 1], list(range(last - 1)), [last]
@@ -476,9 +479,9 @@
         return ((plane == last) & (j < plane - 1)) | ((plane == 0) & (j < planes // 2))
 
     def back(j, p):
-        return (j <= p) & (j + p < planes - 1) & (2 * p >= planes - 2)
-
-    helpable = sorted({j for p in range(last) for j in range(p + 1) if j + p < last and 2 * p >= planes - 2})
+        return (j <= p) & (2 * j < planes) & (2 * p >= planes - 2)
+
+    helpable = [j for j in range(last) if 2 * j < planes]
 
     def helps(j):
         return more & back(j, plane)
@@ -565,7 +568,12 @@
 
     for j in range(planes):
 
-        @pl.when((plane == 0) | helped(j))
+        @pl.when(helped(j))
+        def _():
+            for i in range(2):
+                kv[j, i, :far_rows, :] = jnp.zeros((far_rows, HEAD_DIM), kv.dtype)
+
+        @pl.when(plane == 0)
         def _():
             for i in range(2):
                 kv[j, i, :reach, :] = jnp.zeros((reach, HEAD_DIM), kv.dtype)
@@ -580,15 +588,22 @@
                 base + peers[k],
             )
 
-    def share_q(j):
-        for k in (1, 2, 0):
-            remote(
-                q_ref.at[:, cols(j * PLANE + peers[k])],
-                qs.at[j, place],
-                q_send.at[0],
-                q_recv.at[k, j],
-                base + peers[k],
-            )
+    def share_q(early):
+        def body(j):
+            soon = helped(j) & (role * here < FEW)
+
+            @pl.when(soon if early else jnp.logical_not(soon))
+            def _():
+                for k in (1, 2, 0):
+                    remote(
+                        q_ref.at[:, cols(j * PLANE + peers[k])],
+                        qs.at[j, place],
+                        q_send.at[0],
+                        q_recv.at[k, j],
+                        base + peers[k],
+                    )
+
+        return body
 
     def when_helped(body, truth):
         def step(j):
@@ -693,9 +708,9 @@
         for load in loads:
             load.wait()
     with jax.named_scope("share"):
-        each(when_helped(share_q, True))
+        each(share_q(True))
         each(share)
-        descend(when_helped(share_q, False))
+        descend(share_q(False))
 
     with jax.named_scope("take_core"):
         each(start_core(False))
@@ -710,8 +725,12 @@
         col = lax.broadcasted_iota(jnp.int32, (BLOCK, BLOCK), 1)
         hidden = jnp.full((BLOCK, BLOCK), HIDDEN, jnp.float32)
 
-        def shade(source, target):
-            limit = jnp.where(docs[source] == docs[target], valids[source], 0)
+        def near(first):
+            return docs[first] != docs[first - NEAR - 1]
+
+        def shade(source, target, shown=True):
+            same = (docs[source] == docs[target]) & shown
+            limit = jnp.where(same, valids[source], 0)
             seen = col < limit
             if source == target:
                 seen = seen & (col <= row)
@@ -725,24 +744,33 @@
                     spot = (slice(b * BLOCK, (b + 1) * BLOCK), slice(w * BLOCK, (w + 1) * BLOCK))
                     full = hidden if source > target else shade(source, target)
                     bias[(0, i) + spot] = full
-                    bias[(1, i) + spot] = hidden if source < BACK else full
-        for g in range(BACK):
+                    if source < BACK - NEAR:
+                        bias[(1, i) + spot] = hidden
+                    elif source < BACK and source <= target:
+                        bias[(1, i) + spot] = shade(source, target, near(BACK))
+                    else:
+                        bias[(1, i) + spot] = full
+        for g in range(FEW):
             for c in range(BACK):
                 lower_bias[g * BLOCK : (g + 1) * BLOCK, c * BLOCK : (c + 1) * BLOCK] = shade(
                     BACK + skip + c, BACK + width + g
                 )
         column = lax.broadcasted_iota(jnp.int32, (BLOCK, HEAD_DIM), 0)
 
-    def await_q(j):
+    def await_q(j, early):
         for k in range(PLANE - 1):
-            await_(qs.at[j, rows(peers[k] * here, here)], q_recv.at[k, j])
+            soon = helped(j) & (peers[k] * here < FEW)
+
+            @pl.when(soon if early else jnp.logical_not(soon))
+            def _():
+                await_(qs.at[j, rows(peers[k] * here, here)], q_recv.at[k, j])
 
     await_(qs.at[:, place], local_sem.at[1])
 
     def lower(j):
-        await_q(j)
+        await_q(j, True)
         remote(
-            qs.at[j, pl.ds(0, reach)],
+            qs.at[j, pl.ds(0, few_rows)],
             lower_q.at[j],
             down_send.at[j],
             down_recv.at[j],
@@ -804,18 +832,17 @@
 
             target = lax.fori_loop(0, pairs, earlier, jnp.where(null, counted, 0)) - first
 
-            def mark(b, carry):
-                inside = (first <= b) & (b < end)
-                places_ref[b] = jnp.where(inside, target + b, places_ref[b])
+            def mark(chunk, carry):
+                for step in range(8):
+                    b = chunk * 8 + step
+                    inside = (first <= b) & (b < end)
+                    places_ref[b] = jnp.where(inside, target + b, places_ref[b])
                 return carry
 
-            lax.fori_loop(0, blocks, mark, 0)
+            lax.fori_loop(0, blocks // 8, mark, 0)
             return end
 
         lax.fori_loop(0, order_ref.shape[0], fill, jnp.int32(0))
-
-    with jax.named_scope("map_places"):
-        map_places()
 
     factor = HEAD_DIM ** (-0.5) * math.log2(math.e)
     nt = (((1,), (1,)), ((), ()))
@@ -831,8 +858,9 @@
 
     def help_out(j):
         await_(lower_q.at[j], down_recv.at[j])
-        for first in range(0, BACK, here):
-            count = min(here, BACK - first)
+        send_near = near(BACK + width)
+        for first in range(0, FEW, here):
+            count = min(here, FEW - first)
             lines = slice(first * BLOCK, (first + count) * BLOCK)
             window = pl.ds((BACK + skip + first) * BLOCK, (BACK - first) * BLOCK)
             mixed, peak, total = soften(
@@ -841,14 +869,33 @@
                 kv[j, 1, window, :],
                 lower_bias[lines, first * BLOCK :],
             )
-            part_out[j, lines, :] = (mixed / total).astype(part_out.dtype)
             size = jnp.broadcast_to(peak + jnp.log2(total), (count * BLOCK, BLOCK))
             for b in range(count):
+                g = first + b
                 turned = size[b * BLOCK : (b + 1) * BLOCK].T
-                size_out[j, first + b] = turned[:8]
+                size_out[j, g] = jnp.where(send_near, HIDDEN, turned[:8])
+            mixed = (mixed / total).astype(slot_out.dtype)
+            for b in range(count):
+                side, line = divmod(first + b, NEAR)
+                spot = pl.ds(line * BLOCK, BLOCK)
+                block = kv[j, side, pl.ds((BACK + width - NEAR + line) * BLOCK, BLOCK), :]
+                slot_out[j, side, spot, :] = jnp.where(
+                    send_near, block, mixed[b * BLOCK : (b + 1) * BLOCK]
+                )
+        for g in range(FEW, 2 * NEAR):
+            side, line = divmod(g, NEAR)
+            slot_out[j, side, pl.ds(line * BLOCK, BLOCK), :] = kv[
+                j, side, pl.ds((BACK + width - NEAR + line) * BLOCK, BLOCK), :
+            ]
 
     def send_up(j):
-        remote(part_out.at[j], part_in.at[j], up_send.at[0, j], up_recv.at[0, j], me + PLANE)
+        remote(
+            slot_out.at[j],
+            kv.at[j, :, rows(BACK - NEAR, NEAR)],
+            up_send.at[0, j],
+            up_recv.at[0, j],
+            me + PLANE,
+        )
         remote(size_out.at[j], size_in.at[j], up_send.at[1, j], up_recv.at[1, j], me + PLANE)
 
     def release(j):
@@ -945,10 +992,7 @@
     def own_blocks(t, carry):
         j = last - t
         with jax.named_scope("wait_q"):
-
-            @pl.when(jnp.logical_not(helped(j)))
-            def _():
-                await_q(j)
+            await_q(j, False)
 
         with jax.named_scope("top"):
             simple(j, top)
@@ -1003,7 +1047,7 @@
 
     def merge(j):
         with jax.named_scope("wait_part"):
-            await_(part_in.at[j], up_recv.at[0, j])
+            await_(kv.at[j, :, rows(BACK - NEAR, NEAR)], up_recv.at[0, j])
             await_(size_in.at[j], up_recv.at[1, j])
         with jax.named_scope("merge"):
             for i in range(top - 1, -1, -1):
@@ -1015,13 +1059,15 @@
                 ]
                 for b in range(here):
                     g = i * here + b
-                    if g < BACK:
+                    if g < FEW:
                         size = jnp.broadcast_to(size_in[j, g, :1], (BLOCK, BLOCK)).T
                         mark = peak[b * BLOCK : (b + 1) * BLOCK]
                         high = jnp.maximum(mark, size)
                         mine_share = jnp.exp2(mark - high)
                         their_share = jnp.exp2(size - high)
-                        theirs = part_in[j, g * BLOCK : (g + 1) * BLOCK, :]
+                        side, line = divmod(g, NEAR)
+                        line = (BACK - NEAR + line) * BLOCK
+                        theirs = kv[j, side, line : line + BLOCK, :]
                         mixed[b] = mixed[b] * mine_share + theirs.astype(jnp.float32) * their_share
                         total[b] = total[b] * mine_share + their_share
                 finish(
@@ -1037,6 +1083,9 @@
         def _():
             merge(h)
 
+    with jax.named_scope("map_places"):
+        map_places()
+
     with jax.named_scope("drain"):
         others = features // PLANE * (PLANE - 1)
         await_(own.at[:, :, pl.ds(0, others)], kv_send.at[0])
@@ -1050,7 +1099,7 @@
 
             @pl.when(helps(j))
             def _():
-                await_(part_out.at[j], up_send.at[0, j])
+                await_(slot_out.at[j], up_send.at[0, j])
                 await_(size_out.at[j], up_send.at[1, j])
 
             @pl.when(helped(j))
@@ -1133,7 +1182,7 @@
     anywhere = pl.BlockSpec(memory_space=pl.ANY)
     dma = pltpu.SemaphoreType.DMA
     planes = n // PLANE
-    reach = BACK * BLOCK
+    few = FEW * BLOCK
     cache = jax.ShapeDtypeStruct((1, blocks, part, HEAD_DIM), kind)
     if splits == 1 and here == 2 and planes > 1:
         attended, landed, places = pl.pallas_call(
@@ -1156,12 +1205,11 @@
                 pltpu.VMEM((planes, PLANE * tokens, HEAD_DIM), kind),
                 pltpu.VMEM((planes, PLANE, tokens, HEAD_DIM), kind),
                 pltpu.VMEM((2, PLANE, tokens, (BACK + here) * BLOCK), jnp.float32),
-                pltpu.VMEM((planes, reach, HEAD_DIM), kind),
-                pltpu.VMEM((reach, reach), jnp.float32),
-                pltpu.VMEM((planes, reach, HEAD_DIM), kind),
-                pltpu.VMEM((planes, reach, HEAD_DIM), kind),
-                pltpu.VMEM((planes, BACK, 8, BLOCK), jnp.float32),
-                pltpu.VMEM((planes, BACK, 8, BLOCK), jnp.float32),
+                pltpu.VMEM((planes, few, HEAD_DIM), kind),
+                pltpu.VMEM((few, BACK * BLOCK), jnp.float32),
+                pltpu.VMEM((planes, 2, NEAR * BLOCK, HEAD_DIM), kind),
+                pltpu.VMEM((planes, FEW, 8, BLOCK), jnp.float32),
+                pltpu.VMEM((planes, FEW, 8, BLOCK), jnp.float32),
                 dma((4,)),
                 dma((3,)),
                 dma((3,)),

time: 60.3 us -> 59.7 us (0.990)
  the two profiles are of different devices: /device:TPU:18 before, /device:TPU:0 now
where the time goes in v4:
time: 59.7 us; the launch traced here: 59.6 us
  Pallas kernels  59 us (99%)
  between operations  0.64 us (1%)
    pallas_call x1, Pallas kernels, local(): pl.pallas_call(functools.partial(handoff, n), out_shape=(pltpu.VMEM((toke...  57.3 us
    pallas_call x1, Pallas kernels, local(): pl.pallas_call(publish, out_shape=(jax.ShapeDtypeStruct((tokens, features...  1.65 us

profile of v4, /device:TPU:0, one launch (start us, length us, event | category | flops | bytes accessed | tf_op | source)
XLA Modules:
  0.0 59.6 jit_solution(8219501732242321158)
XLA Ops:
  0.6 57.3 %shard_map.94 = (bf16[256,2048]{1,0:T(8,128)(2,1)S(1)}, bf16[2,4096,128]{2,1,0:T(8,128)(2,1)S(1)}, s32[32]{0:T(128)S(4)}) custom-call(s32[8]{0:T(128)} %counts_hbm.1, s32[16]{0:T(128)} %tails_hbm.1, s32[16]{0:T(128)} %order_hbm.1, s32[8]{0:T(128)} %slot_hbm.1, bf16[256,2048]{1,0:T(8,128)(2,1)} %q_hbm.1, bf16[256,2048]{1,0:T(8,128)(2,1)} %k_hbm.1, ...), custom_call_target="tpu_custom_call" | custom-call | tf_op jit(solution)/shard_map/pallas_call | solution.py:1188
  57.9 1.7 %shard_map.95 = (bf16[256,2048]{1,0:T(8,128)(2,1)}, bf16[1,32,128,128]{3,2,1,0:T(8,128)(2,1)}, bf16[1,32,128,128]{3,2,1,0:T(8,128)(2,1)}) custom-call(s32[32]{0:T(128)S(4)} %get-tuple-element.6.places_ref, bf16[2,4096,128]{2,1,0:T(8,128)(2,1)S(1)} %get-tuple-element.7.landed_ref, bf16[256,2048]{1,0:T(8,128)(2,1)S(1)} %get-tuple-element.8.mixed_ref), custom_call_target="tpu_custom_call" | custom-call | tf_op jit(solution)/shard_map/pallas_call | solution.py:1235

commit v5 on v4

--- a/solution.py
+++ b/solution.py
@@ -381,16 +381,12 @@
     refs = (keys_ref, values_ref)
     part = keys_ref.shape[2]
 
-    def put(b, carry):
+    for b in range(places_ref.shape[0]):
+        place = places_ref[b]
         for kv, ref in enumerate(refs):
             pltpu.make_async_copy(
-                landed_ref.at[kv, pl.ds(pl.multiple_of(b * part, part), part)],
-                ref.at[0, places_ref[b]],
-                out_sem.at[kv],
+                landed_ref.at[kv, b * part : (b + 1) * part], ref.at[0, place], out_sem.at[kv]
             ).start()
-        return carry
-
-    lax.fori_loop(0, places_ref.shape[0], put, 0)
     leave.wait()
     for kv, ref in enumerate(refs):
         pltpu.make_async_copy(ref.at[0], ref.at[0], out_sem.at[kv]).wait()
@@ -423,19 +419,16 @@
     slot_out,
     size_out,
     size_in,
-    small_sem,
     load_sem,
     local_sem,
-    kv_send,
+    leave_sem,
+    share_send,
     kv_recv,
-    q_send,
     q_recv,
     halo_send,
     halo_recv,
     land_send,
-    land_recv,
-    out_send,
-    out_recv,
+    arrive_recv,
     down_send,
     down_recv,
     up_send,
@@ -520,9 +513,7 @@
 
     loads = [
         pltpu.make_async_copy(src, dst, load_sem.at[i])
-        for i, (src, dst) in enumerate(
-            ((k_hbm, own.at[0]), (v_hbm, own.at[1]), (q_hbm, q_ref))
-        )
+        for src, dst, i in ((k_hbm, own.at[0], 0), (v_hbm, own.at[1], 0), (q_hbm, q_ref, 1))
     ]
     barrier = pltpu.get_barrier_semaphore()
     for peer in peers:
@@ -548,7 +539,7 @@
     for load in loads:
         load.start()
     smalls = [
-        pltpu.make_async_copy(src, dst, small_sem.at[i])
+        pltpu.make_async_copy(src, dst, load_sem.at[2 + i])
         for i, (src, dst) in enumerate(
             (
                 (counts_hbm, counts_ref),
@@ -583,7 +574,7 @@
             remote(
                 own.at[:, :, cols(j * PLANE + peers[k])],
                 kv.at[j, :, mine],
-                kv_send.at[0],
+                share_send.at[0],
                 kv_recv.at[k, j],
                 base + peers[k],
             )
@@ -598,8 +589,8 @@
                     remote(
                         q_ref.at[:, cols(j * PLANE + peers[k])],
                         qs.at[j, place],
-                        q_send.at[0],
-                        q_recv.at[k, j],
+                        share_send.at[0],
+                        q_recv.at[0 if early else 1, j],
                         base + peers[k],
                     )
 
@@ -631,8 +622,8 @@
             remote(
                 kv.at[j, :, rows(first, here)],
                 kv.at[j, :, rows(jnp.maximum(rho * here - skip, 0), here)],
-                halo_send.at[j],
-                halo_recv.at[j, rho],
+                halo_send.at[0],
+                halo_recv.at[j],
                 me + PLANE,
             )
 
@@ -641,8 +632,8 @@
             remote(
                 kv.at[j, :, rows(BACK + skip, BACK % here)],
                 kv.at[j, :, rows(0, BACK % here)],
-                halo_send.at[j],
-                halo_recv.at[j, rho],
+                halo_send.at[0],
+                halo_recv.at[j],
                 me + PLANE,
             )
 
@@ -651,8 +642,8 @@
             remote(
                 kv.at[j, :, rows(first, skip % here)],
                 landed_ref.at[:, rows(plane * width + rho * here, skip % here)],
-                land_send.at[1, j],
-                land_recv.at[0],
+                land_send.at[0],
+                arrive_recv.at[0],
                 j * PLANE + role,
             )
 
@@ -661,8 +652,8 @@
             remote(
                 kv.at[j, :, rows(first, here)],
                 landed_ref.at[:, rows(plane * width + rho * here, here)],
-                land_send.at[1, j],
-                land_recv.at[0],
+                land_send.at[0],
+                arrive_recv.at[0],
                 j * PLANE + role,
             )
 
@@ -671,8 +662,8 @@
             remote(
                 kv.at[j, :, rows(first, here)],
                 landed_ref.at[:, rows(plane * width + rho * here, here)],
-                land_send.at[0, j],
-                land_recv.at[0],
+                land_send.at[0],
+                arrive_recv.at[0],
                 j * PLANE + role,
             )
 
@@ -705,8 +696,8 @@
     with jax.named_scope("start_mine"):
         each(start_mine)
     with jax.named_scope("enter_loads"):
-        for load in loads:
-            load.wait()
+        await_(own, load_sem.at[0])
+        await_(q_ref, load_sem.at[1])
     with jax.named_scope("share"):
         each(share_q(True))
         each(share)
@@ -757,13 +748,25 @@
                 )
         column = lax.broadcasted_iota(jnp.int32, (BLOCK, HEAD_DIM), 0)
 
+    soon_roles = -(-FEW // here)
+
     def await_q(j, early):
-        for k in range(PLANE - 1):
-            soon = helped(j) & (peers[k] * here < FEW)
-
-            @pl.when(soon if early else jnp.logical_not(soon))
-            def _():
-                await_(qs.at[j, rows(peers[k] * here, here)], q_recv.at[k, j])
+        def pieces(count, cond):
+            if count > 0:
+
+                @pl.when(cond)
+                def _():
+                    await_(qs.at[j, rows(0, count * here)], q_recv.at[0 if early else 1, j])
+
+        inside = role < soon_roles
+        split = helped(j)
+        if early:
+            pieces(soon_roles - 1, split & inside)
+            pieces(soon_roles, split & jnp.logical_not(inside))
+        else:
+            pieces(PLANE - 1, jnp.logical_not(split))
+            pieces(PLANE - soon_roles, split & inside)
+            pieces(PLANE - 1 - soon_roles, split & jnp.logical_not(inside))
 
     await_(qs.at[:, place], local_sem.at[1])
 
@@ -787,13 +790,7 @@
     each(start_core(True))
 
     def await_halo(j):
-        for rho in range(PLANE):
-            count = min(here, (rho + 1) * here - skip)
-            if count > 0:
-                await_(
-                    kv.at[j, :, rows(max(rho * here - skip, 0), count)],
-                    halo_recv.at[j, rho],
-                )
+        await_(kv.at[j, :, rows(0, BACK)], halo_recv.at[j])
 
     below = rows(jnp.maximum(plane * width - BACK, 0), BACK)
 
@@ -804,8 +801,8 @@
             remote(
                 kv.at[j, :, rows(0, BACK)],
                 landed_ref.at[:, below],
-                land_send.at[2, j],
-                land_recv.at[0],
+                land_send.at[0],
+                arrive_recv.at[0],
                 j * PLANE + role,
             )
 
@@ -888,15 +885,19 @@
                 j, side, pl.ds((BACK + width - NEAR + line) * BLOCK, BLOCK), :
             ]
 
+    def await_up(j, sem):
+        words = FEW * 8 * BLOCK * 2 + 2 * NEAR * BLOCK * HEAD_DIM
+        await_(kv.at[j, 0, pl.ds(0, words // HEAD_DIM)], sem.at[j])
+
     def send_up(j):
         remote(
             slot_out.at[j],
             kv.at[j, :, rows(BACK - NEAR, NEAR)],
-            up_send.at[0, j],
-            up_recv.at[0, j],
+            up_send.at[j],
+            up_recv.at[j],
             me + PLANE,
         )
-        remote(size_out.at[j], size_in.at[j], up_send.at[1, j], up_recv.at[1, j], me + PLANE)
+        remote(size_out.at[j], size_in.at[j], up_send.at[j], up_recv.at[j], me + PLANE)
 
     def release(j):
         @pl.when(hold(j))
@@ -932,20 +933,18 @@
 
     lax.fori_loop(0, planes, far, 0)
 
-    def climb(j, carry):
+    def climb(j):
         @pl.when((plane == 0) & (j > 0))
         def _():
             remote(
                 kv.at[j, :, rows(BACK, skip)],
                 landed_ref.at[:, rows(0, skip)],
-                land_send.at[1, j],
-                land_recv.at[0],
+                land_send.at[0],
+                arrive_recv.at[0],
                 j * PLANE + role,
             )
 
-        return carry
-
-    lax.fori_loop(0, planes, climb, 0)
+    descend(climb)
 
     with jax.named_scope("relay"):
         descend(relay)
@@ -953,7 +952,7 @@
     settle = pltpu.make_async_copy(
         kv.at[plane, :, rows(BACK, width)],
         landed_ref.at[:, rows(plane * width, width)],
-        load_sem.at[0],
+        leave_sem.at[0],
     )
     settle.start()
 
@@ -981,11 +980,11 @@
 
         @pl.when(role == i)
         def _():
-            pltpu.make_async_copy(mixed_ref.at[j, i], target, local_sem.at[2]).start()
+            pltpu.make_async_copy(mixed_ref.at[j, i], target, leave_sem.at[0]).start()
 
         @pl.when(role != i)
         def _():
-            remote(mixed_ref.at[j, i], target, out_send.at[0], out_recv.at[0], base + i)
+            remote(mixed_ref.at[j, i], target, share_send.at[0], arrive_recv.at[0], base + i)
 
     top = PLANE - 1
 
@@ -1031,7 +1030,7 @@
     descend(when_helped(reach_back, False))
 
     settled = pltpu.make_async_copy(
-        kv.at[plane, :, rows(0, BACK)], landed_ref.at[:, below], load_sem.at[1]
+        kv.at[plane, :, rows(0, BACK)], landed_ref.at[:, below], leave_sem.at[0]
     )
 
     @pl.when(late)
@@ -1047,8 +1046,7 @@
 
     def merge(j):
         with jax.named_scope("wait_part"):
-            await_(kv.at[j, :, rows(BACK - NEAR, NEAR)], up_recv.at[0, j])
-            await_(size_in.at[j], up_recv.at[1, j])
+            await_up(j, up_recv)
         with jax.named_scope("merge"):
             for i in range(top - 1, -1, -1):
                 mixed, peak, total = attend(j, i, 1)
@@ -1087,52 +1085,49 @@
         map_places()
 
     with jax.named_scope("drain"):
-        others = features // PLANE * (PLANE - 1)
-        await_(own.at[:, :, pl.ds(0, others)], kv_send.at[0])
-        await_(q_ref.at[:, pl.ds(0, others)], q_send.at[0])
-        await_(q_ref.at[:, pl.ds(0, features // PLANE)], local_sem.at[2])
-
-        def drain(j):
-            @pl.when(more & jnp.logical_not(helps(j)))
+        for h in helpable:
+
+            @pl.when(helps(h))
             def _():
-                await_(kv.at[j, :, rows(0, BACK)], halo_send.at[j])
-
-            @pl.when(helps(j))
+                await_up(h, up_send)
+
+            @pl.when(helped(h))
             def _():
-                await_(slot_out.at[j], up_send.at[0, j])
-                await_(size_out.at[j], up_send.at[1, j])
-
-            @pl.when(helped(j))
+                await_(lower_q.at[h], down_send.at[h])
+
+        for p in range(last):
+
+            @pl.when(plane == p)
             def _():
-                await_(lower_q.at[j], down_send.at[j])
-
-            @pl.when(j < plane)
-            def _():
-                await_(kv.at[j, :, rows(BACK, width)], land_send.at[0, j])
-
-            @pl.when(j > plane)
-            def _():
-                await_(kv.at[j, :, rows(BACK, skip)], land_send.at[1, j])
-
-            @pl.when(late & (j > plane))
-            def _():
-                await_(kv.at[j, :, rows(0, BACK)], land_send.at[2, j])
-
-        each(drain)
-        settle.wait()
-        await_(q_ref.at[:, pl.ds(0, others)], out_send.at[0])
-        await_(q_ref.at[:, pl.ds(0, others)], out_recv.at[0])
+                count = (planes - len([j for j in helpable if j <= p and 2 * p >= planes - 2])) * BACK
+                await_(landed_ref.at[:, rows(0, count)], halo_send.at[0])
+
+        shared = 2 * here * (PLANE - 1)
+        outs = here * planes // 2
+        passed = (planes - 1) * width
+
+        @pl.when(plane == 0)
+        def _():
+            await_(landed_ref.at[:, rows(0, (planes - 1) * skip)], land_send.at[0])
+            await_(landed_ref.at[:, rows(0, width + outs)], leave_sem.at[0])
+
+        @pl.when(late)
+        def _():
+            await_(landed_ref.at[:, rows(0, passed)], land_send.at[0])
+            await_(landed_ref.at[:, rows(0, width + BACK + outs)], leave_sem.at[0])
+
+        await_(kv.at[:, :, rows(0, shared)], share_send.at[0])
 
     with jax.named_scope("land"):
+        others = outs * (PLANE - 1)
 
         @pl.when(late)
         def _():
-            settled.wait()
-            await_(landed_ref.at[:, rows(0, (planes - 1) * width - BACK)], land_recv.at[0])
+            await_(landed_ref.at[:, rows(0, passed - BACK + others)], arrive_recv.at[0])
 
         @pl.when(plane == 0)
         def _():
-            await_(landed_ref.at[:, rows(0, (planes - 1) * width)], land_recv.at[0])
+            await_(kv.at[:, :, rows(0, (passed + others) // planes)], arrive_recv.at[0])
 
 
 def wide_exchange(n, queries, keys, values, block_counts, last_tokens, pack_order):
@@ -1183,6 +1178,7 @@
     dma = pltpu.SemaphoreType.DMA
     planes = n // PLANE
     few = FEW * BLOCK
+    last = planes - 1
     cache = jax.ShapeDtypeStruct((1, blocks, part, HEAD_DIM), kind)
     if splits == 1 and here == 2 and planes > 1:
         attended, landed, places = pl.pallas_call(
@@ -1210,23 +1206,20 @@
                 pltpu.VMEM((planes, 2, NEAR * BLOCK, HEAD_DIM), kind),
                 pltpu.VMEM((planes, FEW, 8, BLOCK), jnp.float32),
                 pltpu.VMEM((planes, FEW, 8, BLOCK), jnp.float32),
-                dma((4,)),
-                dma((3,)),
-                dma((3,)),
+                dma((6,)),
+                dma((2,)),
+                dma((1,)),
                 dma((1,)),
                 dma((PLANE - 1, planes)),
+                dma((2, planes)),
                 dma((1,)),
-                dma((PLANE - 1, planes)),
                 dma((planes,)),
-                dma((planes, PLANE)),
-                dma((3, planes)),
                 dma((1,)),
                 dma((1,)),
-                dma((1,)),
-                dma((planes,)),
-                dma((planes,)),
-                dma((2, planes)),
-                dma((2, planes)),
+                dma((last // 2 + 1,)),
+                dma((last // 2 + 1,)),
+                dma((last // 2 + 1,)),
+                dma((last // 2 + 1,)),
             ],
             compiler_params=pltpu.CompilerParams(
                 collective_id=0, has_side_effects=True, vmem_limit_bytes=60 * 1024 * 1024

time: 59.7 us -> 59.3 us (level)
  no operation moved by 1% of the time
where the time goes in v5:
time: 59.3 us; the launch traced here: 59.1 us
  Pallas kernels  58.5 us (99%)
  between operations  0.64 us (1%)
    pallas_call x1, Pallas kernels, local(): pl.pallas_call(functools.partial(handoff, n), out_shape=(pltpu.VMEM((toke...  56.8 us
    pallas_call x1, Pallas kernels, local(): pl.pallas_call(publish, out_shape=(jax.ShapeDtypeStruct((tokens, features...  1.65 us

profile of v5, /device:TPU:0, one launch (start us, length us, event | category | flops | bytes accessed | tf_op | source)
XLA Modules:
  0.0 59.1 jit_solution(2110845044936184532)
XLA Ops:
  0.6 56.8 %shard_map.94 = (bf16[256,2048]{1,0:T(8,128)(2,1)S(1)}, bf16[2,4096,128]{2,1,0:T(8,128)(2,1)S(1)}, s32[32]{0:T(128)S(4)}) custom-call(s32[8]{0:T(128)} %counts_hbm.1, s32[16]{0:T(128)} %tails_hbm.1, s32[16]{0:T(128)} %order_hbm.1, s32[8]{0:T(128)} %slot_hbm.1, bf16[256,2048]{1,0:T(8,128)(2,1)} %q_hbm.1, bf16[256,2048]{1,0:T(8,128)(2,1)} %k_hbm.1, ...), custom_call_target="tpu_custom_call" | custom-call | tf_op jit(solution)/shard_map/pallas_call | solution.py:1184
  57.5 1.7 %shard_map.95 = (bf16[256,2048]{1,0:T(8,128)(2,1)}, bf16[1,32,128,128]{3,2,1,0:T(8,128)(2,1)}, bf16[1,32,128,128]{3,2,1,0:T(8,128)(2,1)}) custom-call(s32[32]{0:T(128)S(4)} %get-tuple-element.6.places_ref, bf16[2,4096,128]{2,1,0:T(8,128)(2,1)S(1)} %get-tuple-element.7.landed_ref, bf16[256,2048]{1,0:T(8,128)(2,1)S(1)} %get-tuple-element.8.mixed_ref), custom_call_target="tpu_custom_call" | custom-call | tf_op jit(solution)/shard_map/pallas_call | solution.py:1228

commit v6 on v5

--- a/solution.py
+++ b/solution.py
@@ -471,6 +471,9 @@
     def hold(j):
         return ((plane == last) & (j < plane - 1)) | ((plane == 0) & (j < planes // 2))
 
+    def defer(j):
+        return (plane == last) & (j > 0) & (j < plane - 1)
+
     def back(j, p):
         return (j <= p) & (2 * j < planes) & (2 * p >= planes - 2)
 
@@ -900,7 +903,7 @@
         remote(size_out.at[j], size_in.at[j], up_send.at[j], up_recv.at[j], me + PLANE)
 
     def release(j):
-        @pl.when(hold(j))
+        @pl.when(hold(j) & jnp.logical_not(defer(j)))
         def _():
             forward(j, role)
             forward(j, peers[0])
@@ -910,7 +913,10 @@
         with jax.named_scope("take_far"):
             for k in (1, 2):
                 take(k, j)
-                forward(j, peers[k])
+
+                @pl.when(jnp.logical_not(defer(j)))
+                def _():
+                    forward(j, peers[k])
 
         @pl.when(t == min(1, last))
         def _():
@@ -988,23 +994,18 @@
 
     top = PLANE - 1
 
-    def own_blocks(t, carry):
-        j = last - t
-        with jax.named_scope("wait_q"):
-            await_q(j, False)
-
-        with jax.named_scope("top"):
-            simple(j, top)
-
-            @pl.when(t > 0)
-            def _():
-                give(jnp.minimum(j + 1, last), top)
-
-        return carry
-
-    lax.fori_loop(0, planes, own_blocks, 0)
-
-    def reach_back(j):
+    def lump(j):
+        @pl.when(defer(j))
+        def _():
+            remote(
+                kv.at[j, :, rows(BACK, width)],
+                landed_ref.at[:, rows(plane * width, width)],
+                land_send.at[0],
+                arrive_recv.at[0],
+                j * PLANE + role,
+            )
+
+    def reach_back(j, waiting):
         with jax.named_scope("wait_halo"):
 
             @pl.when(late & (j <= plane))
@@ -1015,19 +1016,45 @@
             for i in range(top - 1, -1, -1):
                 simple(j, i)
                 if i == top - 1:
-
-                    @pl.when(j == last)
-                    def _():
-                        give(0, top)
-
-                    @pl.when(j < last)
-                    def _():
-                        give(jnp.minimum(j + 1, last), 0)
-
+                    give(*waiting)
                 else:
                     give(j, i + 1)
 
-    descend(when_helped(reach_back, False))
+    def one_head(t, carry):
+        j = last - t
+        with jax.named_scope("wait_q"):
+            await_q(j, False)
+        with jax.named_scope("top"):
+            simple(j, top)
+
+            @pl.when(t == min(1, last))
+            def _():
+                descend(lump)
+
+        before = jnp.minimum(j + 1, last)
+        earlier = jnp.minimum(j + 2, last)
+        full = jnp.logical_not(helped(earlier))
+
+        @pl.when((t > 1) & full)
+        def _():
+            give(earlier, 0)
+
+        @pl.when((t == 1) | ((t > 1) & jnp.logical_not(full)))
+        def _():
+            give(before, top)
+
+        @pl.when((t > 0) & jnp.logical_not(helped(before)))
+        def _():
+            reach_back(before, (j, top))
+
+        return carry
+
+    lax.fori_loop(0, planes, one_head, 0)
+    whole = jnp.logical_not(helped(0))
+
+    @pl.when(whole)
+    def _():
+        reach_back(0, (1, 0))
 
     settled = pltpu.make_async_copy(
         kv.at[plane, :, rows(0, BACK)], landed_ref.at[:, below], leave_sem.at[0]
@@ -1037,12 +1064,17 @@
     def _():
         settled.start()
 
-    for j in range(planes):
-        first = jnp.logical_not(helped(j))
-
-        @pl.when(first & helped(j - 1) if j else first)
-        def _():
-            give(j, 0)
+    @pl.when(whole)
+    def _():
+        give(0, 0)
+
+    @pl.when(helped(0) & jnp.logical_not(helped(1)))
+    def _():
+        give(1, 0)
+
+    @pl.when(helped(0) & helped(1))
+    def _():
+        give(0, top)
 
     def merge(j):
         with jax.named_scope("wait_part"):

time: 59.3 us -> 57.6 us (0.971)
  the two profiles are of different devices: /device:TPU:0 before, /device:TPU:18 now
where the time goes in v6:
time: 57.6 us; the launch traced here: 57 us
  Pallas kernels  56.4 us (98%)
  between operations  0.64 us (1%)
    pallas_call x1, Pallas kernels, local(): pl.pallas_call(functools.partial(handoff, n), out_shape=(pltpu.VMEM((toke...  54.7 us
    pallas_call x1, Pallas kernels, local(): pl.pallas_call(publish, out_shape=(jax.ShapeDtypeStruct((tokens, features...  1.65 us

profile of v6, /device:TPU:18, one launch (start us, length us, event | category | flops | bytes accessed | tf_op | source)
XLA Modules:
  0.0 57.0 jit_solution(2646769470509338405)
XLA Ops:
  0.6 54.7 %shard_map.94 = (bf16[256,2048]{1,0:T(8,128)(2,1)S(1)}, bf16[2,4096,128]{2,1,0:T(8,128)(2,1)S(1)}, s32[32]{0:T(128)S(4)}) custom-call(s32[8]{0:T(128)} %counts_hbm.1, s32[16]{0:T(128)} %tails_hbm.1, s32[16]{0:T(128)} %order_hbm.1, s32[8]{0:T(128)} %slot_hbm.1, bf16[256,2048]{1,0:T(8,128)(2,1)} %q_hbm.1, bf16[256,2048]{1,0:T(8,128)(2,1)} %k_hbm.1, ...), custom_call_target="tpu_custom_call" | custom-call | tf_op jit(solution)/shard_map/pallas_call | solution.py:1216
  55.4 1.7 %shard_map.95 = (bf16[256,2048]{1,0:T(8,128)(2,1)}, bf16[1,32,128,128]{3,2,1,0:T(8,128)(2,1)}, bf16[1,32,128,128]{3,2,1,0:T(8,128)(2,1)}) custom-call(s32[32]{0:T(128)S(4)} %get-tuple-element.6.places_ref, bf16[2,4096,128]{2,1,0:T(8,128)(2,1)S(1)} %get-tuple-element.7.landed_ref, bf16[256,2048]{1,0:T(8,128)(2,1)S(1)} %get-tuple-element.8.mixed_ref), custom_call_target="tpu_custom_call" | custom-call | tf_op jit(solution)/shard_map/pallas_call | solution.py:1260

commit v7 on v6

--- a/solution.py
+++ b/solution.py
@@ -813,12 +813,6 @@
         pairs = counts_ref.shape[0]
         blocks = places_ref.shape[0]
 
-        def empty(b, carry):
-            places_ref[b] = 0
-            return carry
-
-        lax.fori_loop(0, blocks, empty, 0)
-
         def fill(i, first):
             prompt = order_ref[i]
             pair = lax.rem(prompt, pairs)
@@ -908,6 +902,15 @@
             forward(j, role)
             forward(j, peers[0])
 
+    def empty_places():
+        def empty(b, carry):
+            places_ref[b] = 0
+            return carry
+
+        lax.fori_loop(0, places_ref.shape[0], empty, 0)
+
+    empty_places()
+
     def far(t, carry):
         j = turn(t)
         with jax.named_scope("take_far"):
@@ -933,6 +936,7 @@
 
             @pl.when(helps(h) & (j == h))
             def _():
+                empty_places()
                 send_up(h)
 
         return carry
@@ -1063,6 +1067,8 @@
     @pl.when(late)
     def _():
         settled.start()
+
+    empty_places()
 
     @pl.when(whole)
     def _():
@@ -1105,6 +1111,7 @@
                 )
                 if i < top - 1:
                     give(j, i + 1)
+        empty_places()
         give(j, 0)
 
     for h in helpable:
@@ -1115,6 +1122,7 @@
 
     with jax.named_scope("map_places"):
         map_places()
+
 
     with jax.named_scope("drain"):
         for h in helpable:

time: 57.6 us -> 57.6 us (level)
  no operation moved by 1% of the time
where the time goes in v7:
time: 57.6 us; the launch traced here: 56.8 us
  Pallas kernels  56.1 us (97%)
  between operations  0.64 us (1%)
    pallas_call x1, Pallas kernels, local(): pl.pallas_call(functools.partial(handoff, n), out_shape=(pltpu.VMEM((toke...  54.5 us
    pallas_call x1, Pallas kernels, local(): pl.pallas_call(publish, out_shape=(jax.ShapeDtypeStruct((tokens, features...  1.65 us

profile of v7, /device:TPU:18, one launch (start us, length us, event | category | flops | bytes accessed | tf_op | source)
XLA Modules:
  0.0 56.8 jit_solution(3775713859267623781)
XLA Ops:
  0.6 54.5 %shard_map.94 = (bf16[256,2048]{1,0:T(8,128)(2,1)S(1)}, bf16[2,4096,128]{2,1,0:T(8,128)(2,1)S(1)}, s32[32]{0:T(128)S(4)}) custom-call(s32[8]{0:T(128)} %counts_hbm.1, s32[16]{0:T(128)} %tails_hbm.1, s32[16]{0:T(128)} %order_hbm.1, s32[8]{0:T(128)} %slot_hbm.1, bf16[256,2048]{1,0:T(8,128)(2,1)} %q_hbm.1, bf16[256,2048]{1,0:T(8,128)(2,1)} %k_hbm.1, ...), custom_call_target="tpu_custom_call" | custom-call | tf_op jit(solution)/shard_map/pallas_call | solution.py:1224
  55.1 1.7 %shard_map.95 = (bf16[256,2048]{1,0:T(8,128)(2,1)}, bf16[1,32,128,128]{3,2,1,0:T(8,128)(2,1)}, bf16[1,32,128,128]{3,2,1,0:T(8,128)(2,1)}) custom-call(s32[32]{0:T(128)S(4)} %get-tuple-element.6.places_ref, bf16[2,4096,128]{2,1,0:T(8,128)(2,1)S(1)} %get-tuple-element.7.landed_ref, bf16[256,2048]{1,0:T(8,128)(2,1)S(1)} %get-tuple-element.8.mixed_ref), custom_call_target="tpu_custom_call" | custom-call | tf_op jit(solution)/shard_map/pallas_call | solution.py:1268
